TPU v7x, 256 devices: a whole 4x4x8 slice. The times are simulated.
256 devices in a mesh: row: 16 (over x, y), col: 16 (over z, core).
Axes of the slice: x: 4, y: 4, z: 8, core: 2. Of those that a mesh axis runs over, the one named last changes fastest.
Arguments:
- wrapped: float32 [1, 16384, 16384], P(None, 'row', 'col'), may hold values from -2.8 to 2.8
- col_steps: int32 [1, 16, 16], P(None, 'row', 'col'), may hold values from -2 to 2, as said below
- row_steps: int32 [1, 16, 16], P(None, 'row', 'col'), may hold values from -2 to 2, as said below
Outputs:
- unwrapped: float32 [1, 16384, 16384], P(None, 'row', 'col')
Inputs may be any that keep to these rules, and one draw needn't show every extreme that they name: `col_steps`: nonzero whole numbers; the last tile column has no edge. `row_steps`: nonzero whole numbers; the last tile row has no edge.
All inputs are finite; a program needn't handle non-finite values.
Results may differ from a plain program's by a relative error of at most 0.0003.
Values sent between devices are 32-bit elements; how exact they have to be, the bound alone decides.
A program may use at most 64 MiB of HBM per device.

v0:
```python
import math

import jax
import jax.numpy as jnp
from jax import lax
from jax.sharding import PartitionSpec as P

ITERS = 2


TWO_PI = 2.0 * math.pi


def with_halo(x, sides, width):
    edges = {}
    for axis, dim in sides:
        peers, length = (lax.axis_size(axis), x.shape[dim])
        up = [(i, (i + 1) % peers) for i in range(peers - 1)]
        last = lax.slice_in_dim(x, length - width, length, axis=dim)
        leading = lax.slice_in_dim(x, 0, width, axis=dim)
        edges[dim] = (
            lax.ppermute(last, axis, up),
            lax.ppermute(leading, axis, [(b, a) for a, b in up]),
        )
    done = []
    for _, dim in sides:
        low, high = edges[dim]
        around = [(width, width) if d in done else (0, 0) for d in range(x.ndim)]
        x = jnp.concatenate([jnp.pad(low, around), x, jnp.pad(high, around)], axis=dim)
        done.append(dim)
    return x


def gather_turned(arrays, axis, dims):
    turned = [jnp.moveaxis(a, dim, 0) for a, dim in zip(arrays, dims)]
    both = jnp.concatenate([t.reshape(len(t), -1) for t in turned], axis=1)
    result, at, finished = (lax.all_gather(both, axis, axis=0, tiled=True), 0, [])
    for t, dim in zip(turned, dims):
        piece = result[:, at : at + t[0].size].reshape(-1, *t.shape[1:])
        finished.append(jnp.moveaxis(piece, 0, dim))
        at += t[0].size
    return tuple(finished)


def wrap_diff(change):
    return change - TWO_PI * jnp.floor(change / TWO_PI + 0.5)


def running_sum(values):
    frames, tile_rows, tile_width = values.shape
    block_len = math.gcd(tile_width, 128)
    blocks_in = tile_width // block_len
    pieces = values.reshape(frames, tile_rows, blocks_in, block_len)
    strict_upper = (
        lax.broadcasted_iota(jnp.int32, (block_len, block_len), 0)
        < lax.broadcasted_iota(jnp.int32, (block_len, block_len), 1)
    ).astype(jnp.float32)
    inside = jnp.einsum("frcm,mk->frck", pieces, strict_upper, precision=lax.Precision.HIGHEST)
    totals = jnp.sum(pieces, axis=3)
    before = jnp.cumsum(totals, axis=2) - totals
    return (inside + before[:, :, :, None]).reshape(frames, tile_rows, tile_width)


def integrate_line(line):
    steps = wrap_diff(line[:, 1:] - line[:, :-1])
    running = jnp.cumsum(steps, axis=1)
    return line[:, 0:1] + jnp.concatenate([jnp.zeros_like(line[:, 0:1]), running], axis=1)


def mean_jump(own_edge, crossing, beyond, weights):
    return jnp.sum(weights * (own_edge + crossing - beyond), axis=1) / jnp.sum(weights, axis=1)


def on_device(wrapped, col_steps, row_steps):
    frames, tile_rows, tile_cols = wrapped.shape
    padded = with_halo(wrapped, (("row", 1), ("col", 2)), 1)
    step_x = wrap_diff(padded[:, :, 1:] - padded[:, :, :-1])
    step_y = wrap_diff(padded[:, 1:, :] - padded[:, :-1, :])
    charge_across = (
        step_x[:, 0:tile_rows, tile_cols - 1]
        + step_y[:, 0:tile_rows, tile_cols]
        - step_x[:, 1 : tile_rows + 1, tile_cols - 1]
        - step_y[:, 0:tile_rows, tile_cols - 1]
    ) / TWO_PI
    at_top = (lax.broadcasted_iota(jnp.int32, (1, tile_rows), 1) == 0) & (
        lax.axis_index("row") == 0
    )
    charge_across = jnp.where(at_top, 0.0, charge_across)
    charge_down = (
        step_x[:, tile_rows - 1, 0:tile_cols]
        + step_y[:, tile_rows - 1, 1 : tile_cols + 1]
        - step_x[:, tile_rows, 0:tile_cols]
        - step_y[:, tile_rows - 1, 0:tile_cols]
    ) / TWO_PI
    at_left = (lax.broadcasted_iota(jnp.int32, (1, tile_cols), 1) == 0) & (
        lax.axis_index("col") == 0
    )
    charge_down = jnp.where(at_left, 0.0, charge_down)
    weight_across = 1.0 / (1.0 + jnp.abs(charge_across))
    weight_down = 1.0 / (1.0 + jnp.abs(charge_down))
    crossing_x = step_x[:, 1 : tile_rows + 1, tile_cols]
    crossing_y = step_y[:, tile_rows, 1 : tile_cols + 1]
    column_steps = step_y[:, 1 : tile_rows + 1, 1]
    downward = jnp.cumsum(column_steps, axis=1) - column_steps
    anchor = wrapped[:, 0, 0]
    integrated = (anchor[:, None] + downward)[:, :, None] + running_sum(
        step_x[:, 1 : tile_rows + 1, 1 : tile_cols + 1]
    )
    cycles_across = TWO_PI * col_steps[:, 0, 0].astype(jnp.float32)
    cycles_down = TWO_PI * row_steps[:, 0, 0].astype(jnp.float32)
    right_first = integrate_line(padded[:, 1 : tile_rows + 1, tile_cols + 1])
    below_first = integrate_line(padded[:, tile_rows + 1, 1 : tile_cols + 1])
    base_across = (
        mean_jump(integrated[:, :, -1], crossing_x, right_first, weight_across) + cycles_across
    )
    base_down = mean_jump(integrated[:, -1, :], crossing_y, below_first, weight_down) + cycles_down
    grid_rows = lax.axis_size("row")
    grid_cols = lax.axis_size("col")
    every_across, every_down = gather_turned(
        (base_across[:, None], base_down[:, None]), ("row", "col"), (1, 1)
    )
    every_across = every_across.reshape(frames, grid_rows, grid_cols)
    every_down = every_down.reshape(frames, grid_rows, grid_cols)
    totals = jnp.zeros((frames, grid_rows, grid_cols), jnp.float32)
    for sweep in range(ITERS):
        right_total = jnp.concatenate(
            [totals[:, :, 1:], jnp.zeros((frames, grid_rows, 1), jnp.float32)], axis=2
        )
        below_total = jnp.concatenate(
            [totals[:, 1:, :], jnp.zeros((frames, 1, grid_cols), jnp.float32)], axis=1
        )
        horizontal = every_across + totals - right_total
        vertical = every_down + totals - below_total
        prefix_across = jnp.cumsum(horizontal, axis=2) - horizontal
        prefix_down = jnp.cumsum(vertical, axis=1) - vertical
        totals = totals + 0.5 * (
            prefix_across + prefix_across[:, 0:1, :] + prefix_down + prefix_down[:, :, 0:1]
        )
    mine = lax.dynamic_slice(
        totals, (0, lax.axis_index("row"), lax.axis_index("col")), (frames, 1, 1)
    )
    return (integrated + mine) / TWO_PI


def solution(mesh):
    in_specs = (P(None, "row", "col"), P(None, "row", "col"), P(None, "row", "col"))
    out_specs = P(None, "row", "col")
    return jax.shard_map(
        on_device, mesh=mesh, in_specs=in_specs, out_specs=out_specs, check_vma=False
    )
```

profile of v0, /device:TPU:1, one launch (start us, length us, event | category | flops | bytes accessed | tf_op | source)
XLA Modules:
  0.0 165.0 jit_solution(7441537384304579443)
XLA Ops:
  0.0 0.8 fusion.18
  1.0 4.1 %collective-permute-start.1 = (f32[1,1,1024]{1,2,0:T(8,128)S(1)}, f32[1,1,1024]{1,2,0:T(8,128)S(1)}, u32[]{:S(2)}, u32[]{:S(2)}) collective-permute-start(f32[1,1,1024]{1,2,0:T(8,128)S(1)} %copy.21), channel_id=1, source_target_pairs={{0,16},{16,32},{32,48},{48,64},{64,80},{80,96},{96,112},{112,128},... | collective-permute-start | bytes 12296 | tf_op jit(solution)/shard_map/ppermute | solution.py:22
  5.3 1.3 collective-permute-start.2
  6.6 5.3 %copy.20 = f32[1,1024,1024]{1,2,0:T(8,128)} copy(f32[1,1024,1024]{2,1,0:T(8,128)} %param.3) | data formatting | bytes 8388608 | tf_op args[0]
  11.9 0.8 fusion.17
  12.7 2.9 %collective-permute-start.3 = (f32[1,1024,1]{1,2,0:T(1,128)S(1)}, f32[1,1024,1]{1,2,0:T(1,128)S(1)}, u32[]{:S(2)}, u32[]{:S(2)}) collective-permute-start(f32[1,1024,1]{1,2,0:T(1,128)S(1)} %get-tuple-element.13), channel_id=1, source_target_pairs={{1,0},{2,1},{3,2},{4,3},{5,4},{6,5},{7,6},{8,7},{9,8},{10,9},{11,1... | collective-permute-start | bytes 12296 | tf_op jit(solution)/shard_map/ppermute | solution.py:23
  15.6 3.4 %collective-permute-start = (f32[1,1024,1]{1,2,0:T(1,128)S(1)}, f32[1,1024,1]{1,2,0:T(1,128)S(1)}, u32[]{:S(2)}, u32[]{:S(2)}) collective-permute-start(f32[1,1024,1]{1,2,0:T(1,128)S(1)} %get-tuple-element.14), channel_id=1, source_target_pairs={{0,1},{1,2},{2,3},{3,4},{4,5},{5,6},{6,7},{7,8},{8,9},{9,10},{10,1... | collective-permute-start | bytes 12296 | tf_op jit(solution)/shard_map/ppermute | solution.py:22
  19.1 1.3 slice.130
  22.0 0.6 slice.192
  22.6 0.5 slice.183
  23.2 6.4 %concatenate.59 = f32[1,1026,1024]{1,2,0:T(8,128)} concatenate(f32[1,1,1024]{1,2,0:T(8,128)S(1)} %collective-permute-done.1, f32[1,1024,1024]{1,2,0:T(8,128)} %copy.20, f32[1,1,1024]{1,2,0:T(8,128)S(1)} %collective-permute-done.2), dimensions={1} | concatenate | bytes 8404992 | tf_op jit(solution)/shard_map/concatenate | solution.py:29
  29.7 7.4 %multiply_subtract_fusion = f32[1,1026,1025]{1,2,0:T(8,128)} fusion(f32[1,1026,1024]{1,2,0:T(8,128)} %concatenate.59, f32[1,1026,1]{1,2,0:T(1,128)S(1)} %pad.15, f32[1,1026,1]{1,2,0:T(1,128)S(1)} %pad.16), kind=kLoop, calls=%fused_computation.2 | loop fusion | flops 8413200 | bytes 8417304 | tf_op jit(solution)/shard_map/sub | solution.py:46
  37.0 15.3 %concatenate.60 = f32[1,1026,1026]{1,2,0:T(8,128)} concatenate(f32[1,1026,1]{1,2,0:T(1,128)S(1)} %pad.15, f32[1,1026,1024]{1,2,0:T(8,128)} %concatenate.59, f32[1,1026,1]{1,2,0:T(1,128)S(1)} %pad.16), dimensions={2} | concatenate | bytes 8421408 | tf_op jit(solution)/shard_map/concatenate | solution.py:29
  52.3 0.3 reduce-window.26
  53.0 0.3 reduce-window.24
  53.6 5.1 %multiply_subtract_fusion.1 = f32[1,1025,1026]{1,2,0:T(8,128)S(1)} fusion(f32[1,1026,1026]{1,2,0:T(8,128)} %concatenate.60), kind=kLoop, calls=%fused_computation.3 | loop fusion | flops 6309900 | bytes 12619800 | tf_op jit(solution)/shard_map/sub | solution.py:46
  58.8 2.2 %copy-done.1 = f32[1,1025,1026]{1,2,0:T(8,128)} copy-done((f32[1,1025,1026]{1,2,0:T(8,128)}, f32[1,1025,1026]{1,2,0:T(8,128)S(1)}, u32[]{:S(2)}) %copy-start.1) | copy-done | bytes 4206624
  61.7 5.7 %slice.176 = f32[1,1024,1024]{1,2,0:T(8,128)} slice(f32[1,1026,1025]{1,2,0:T(8,128)} %multiply_subtract_fusion), slice={[0:1], [1:1025], [1:1025]} | slice | bytes 8388608 | tf_op jit(solution)/shard_map/slice | solution.py:107
  67.4 2.6 %reduce_sum.45 = f32[1024,8]{0,1:T(8,128)S(1)} reduce(f32[1024,8,128]{0,2,1:T(8,128)} %bitcast.62, f32[]{:T(128)} %constant.51.clone.1), dimensions={2}, to_apply=%region_2.3 | reduce | flops 1040384 | bytes 4227076 | tf_op jit(solution)/shard_map/reduce_sum | solution.py:59
  70.1 5.3 %convolution_add_fusion = f32[1024,8,128]{0,2,1:T(8,128)S(1)} fusion(f32[1024,8,128]{0,2,1:T(8,128)} %bitcast.63, f32[1024,8]{0,1:T(8,128)S(1)} %sub.200), kind=kOutput, calls=%fused_computation.6 | convolution fusion | flops 1611677696 | bytes 8421376 | tf_op jit(solution)/shard_map/frcm,mk->frck/dot_general | solution.py:58
  75.4 1.5 subtract_add_fusion
  77.0 0.8 bitcast_add_fusion
  77.8 2.6 %fusion = (f32[1024]{0:T(1024)S(1)}, f32[1024]{0:T(1024)S(1)}) fusion(f32[1,1025,1026]{1,2,0:T(8,128)} %copy-done.1, f32[1,1024,1024]{1,2,0:T(8,128)S(1)} %bitcast_add_fusion, f32[1,1026,1025]{1,2,0:T(8,128)} %multiply_subtract_fusion), kind=kLoop, calls=%fused_computation.8 | loop fusion | flops 5120 | bytes 32768 | tf_op jit(solution)/shard_map/add | solution.py:71
  80.6 2.9 %fusion.15 = (f32[]{:T(128)}, f32[]{:T(128)}, f32[]{:T(128)}, f32[]{:T(128)}) fusion(f32[1,1023]{1,0:T(1,128)S(1)} %slice_add_fusion.3, f32[1,1]{1,0:T(1,128)} %constant.59.clone.1, f32[]{:T(128)} %bitcast.12, f32[1,1026,1025]{1,2,0:T(8,128)} %multiply_subtract_fusion, f32[1,1024,1024]{1,2,0:T(8,128)S(1)} %bitcast_add_fusion, f32[1,1025,1026]{1,2,0:T(8,128)} %copy-done.1, ...), kind=kLoop, calls=%fused_computation.62 | loop fusion | flops 28668 | bytes 40982 | tf_op jit(solution)/shard_map/reduce_sum | solution.py:71
  86.2 60.9 %all-gather = f32[256,1,2]{2,1,0:T(1,128)S(1)} all-gather(f32[1,1,2]{2,1,0:T(1,128)S(1)} %maximum_bitcast_fusion), channel_id=1, replica_groups=mesh['row'=16,'col'=16] {'row','col'}, dimensions={0}, use_global_device_ids=true | all-gather | bytes 2056 | tf_op jit(solution)/shard_map/all_gather | solution.py:37
  148.4 0.7 dynamic-slice.1
  149.1 0.6 dynamic-slice
  149.6 1.2 fusion.19
  150.8 1.2 fusion.20
  153.4 0.6 fusion.21
  154.0 5.7 %add_multiply_fusion = f32[1,1024,1024]{1,2,0:T(8,128)} fusion(f32[]{:T(128)} %bitcast.32, f32[1024,8,128]{0,2,1:T(8,128)} %copy-done, f32[1024]{0:T(1024)S(1)} %bitcast.66), kind=kLoop, calls=%fused_computation.5 | loop fusion | flops 3145728 | bytes 8392708 | tf_op jit(solution)/shard_map/div | solution.py:142
  159.7 5.3 %copy.26 = f32[1,1024,1024]{2,1,0:T(8,128)} copy(f32[1,1024,1024]{1,2,0:T(8,128)} %add_multiply_fusion) | data formatting | bytes 8388608 | tf_op jit(solution)/shard_map/div | solution.py:142
  (54 shorter events, 4.0 us)
Async XLA Ops:
  1.0 22.1 %collective-permute-start.1 = (f32[1,1,1024]{1,2,0:T(8,128)S(1)}, f32[1,1,1024]{1,2,0:T(8,128)S(1)}, u32[]{:S(2)}, u32[]{:S(2)}) collective-permute-start(f32[1,1,1024]{1,2,0:T(8,128)S(1)} %copy.21), channel_id=1, source_target_pairs={{0,16},{16,32},{32,48},{48,64},{64,80},{80,96},{96,112},{112,128},... | collective-permute-start | bytes 12296 | tf_op jit(solution)/shard_map/ppermute | solution.py:22
  5.3 16.3 %collective-permute-start.2 = (f32[1,1,1024]{1,2,0:T(8,128)S(1)}, f32[1,1,1024]{1,2,0:T(8,128)S(1)}, u32[]{:S(2)}, u32[]{:S(2)}) collective-permute-start(f32[1,1,1024]{1,2,0:T(8,128)S(1)} %copy.22), channel_id=1, source_target_pairs={{16,0},{32,16},{48,32},{64,48},{80,64},{96,80},{112,96},{128,112},... | collective-permute-start | bytes 12296 | tf_op jit(solution)/shard_map/ppermute | solution.py:23
  12.7 9.2 %collective-permute-start.3 = (f32[1,1024,1]{1,2,0:T(1,128)S(1)}, f32[1,1024,1]{1,2,0:T(1,128)S(1)}, u32[]{:S(2)}, u32[]{:S(2)}) collective-permute-start(f32[1,1024,1]{1,2,0:T(1,128)S(1)} %get-tuple-element.13), channel_id=1, source_target_pairs={{1,0},{2,1},{3,2},{4,3},{5,4},{6,5},{7,6},{8,7},{9,8},{10,9},{11,1... | collective-permute-start | bytes 12296 | tf_op jit(solution)/shard_map/ppermute | solution.py:23
  15.6 14.0 %collective-permute-start = (f32[1,1024,1]{1,2,0:T(1,128)S(1)}, f32[1,1024,1]{1,2,0:T(1,128)S(1)}, u32[]{:S(2)}, u32[]{:S(2)}) collective-permute-start(f32[1,1024,1]{1,2,0:T(1,128)S(1)} %get-tuple-element.14), channel_id=1, source_target_pairs={{0,1},{1,2},{2,3},{3,4},{4,5},{5,6},{6,7},{7,8},{8,9},{9,10},{10,1... | collective-permute-start | bytes 12296 | tf_op jit(solution)/shard_map/ppermute | solution.py:22
  58.7 2.2 %copy-start.1 = (f32[1,1025,1026]{1,2,0:T(8,128)}, f32[1,1025,1026]{1,2,0:T(8,128)S(1)}, u32[]{:S(2)}) copy-start(f32[1,1025,1026]{1,2,0:T(8,128)S(1)} %multiply_subtract_fusion.1) | copy-start | bytes 12619804
  75.4 5.1 %copy-start = (f32[1024,8,128]{0,2,1:T(8,128)}, f32[1024,8,128]{0,2,1:T(8,128)S(1)}, u32[]{:S(2)}) copy-start(f32[1024,8,128]{0,2,1:T(8,128)S(1)} %convolution_add_fusion) | copy-start | bytes 12582916
where the time goes:
time: 166 us; the launch traced here: 165 us
  blocking collectives  60.9 us (37%)
  local copies, waits for them, and re-layouts  47.6 us (29%)
  other arithmetic  34.1 us (21%)
  starting transfers between devices  11.6 us (7%)
  between operations  5.5 us (3%)
  matrix products  5.29 us (3%)
    all_gather x1, blocking collectives, gather_turned(): lax.all_gather(both, axis, axis=0, tiled=True)  60.9 us
    concatenate x2, local copies, waits for them, and re-layouts, with_halo(): jnp.concatenate([jnp.pad(low, around), x, jnp.pad(high, around)], axis=dim)  21.6 us
    sub x4, other arithmetic, wrap_diff(): return change - TWO_PI * jnp.floor(change / TWO_PI + 0.5)  12.6 us
    unnamed x5, local copies, waits for them, and re-layouts  7.52 us
    ppermute x2, starting transfers between devices, with_halo(): lax.ppermute(last, axis, up)  7.49 us
    slice x1, local copies, waits for them, and re-layouts, on_device(): step_x[:, 1:tile_rows + 1, 1:tile_cols + 1]  5.75 us
    div x1, other arithmetic, on_device(): return (integrated + mine) / TWO_PI  5.7 us
    div x1, local copies, waits for them, and re-layouts, on_device(): return (integrated + mine) / TWO_PI  5.34 us
  transfers between devices with their start and end apart: 4, of which 0 were waited for; matrix products, arithmetic and copies ran while one was open for 9% of the time, Pallas kernels for 0%

commit v1 on v0

v1 whole, which is shorter than its diff:
```python
import functools
import math

import jax
import jax.numpy as jnp
from jax import lax
from jax.experimental import pallas as pl
from jax.experimental.pallas import tpu as pltpu
from jax.sharding import PartitionSpec as P

ITERS = 2
PER_CYCLE = 1.0 / (2.0 * math.pi)
MESH = pl.DeviceIdType.MESH
LANES = 128
STRIP = 32


def turns(change):
    return jnp.floor(change * PER_CYCLE + 0.5)


def positions(shape):
    return lax.broadcasted_iota(jnp.int32, shape, 0), lax.broadcasted_iota(jnp.int32, shape, 1)


def before(line, first):
    sub, lane = positions(line.shape)
    along = pltpu.roll(line, 1, 1)
    moved = jnp.where(lane == 0, pltpu.roll(along, 1, 0), along)
    return jnp.where((lane == 0) & (sub == 0), first, moved)


def line_turns(line):
    return turns(line - before(line, line))


def edge_weight(inner, outer, inner_first, outer_first, no_first):
    sub, lane = positions(inner.shape)
    cross = turns(outer - inner)
    cross_before = before(cross, turns(outer_first - inner_first))
    along_inner = turns(inner - before(inner, inner_first))
    along_outer = turns(outer - before(outer, outer_first))
    charge = jnp.abs(cross_before - cross + along_outer - along_inner)
    charge = jnp.where((lane == 0) & (sub == 0) & no_first, 0.0, charge)
    return 1.0 / (1.0 + charge)


def total(x):
    return jnp.sum(jnp.sum(x, axis=1, keepdims=True), axis=0, keepdims=True)


def kernel(
    n_row, n_col, wrapped, col_steps, row_steps, pre, offset,
    x, m, acc, mcol, tri, top, corner, own_col, own_last, beyond_col, below, corner_up, corner_left,
    jump_x, jump_y, seen_x, seen_y, sum_x, sum_y, first_x, first_y,
    in_sem, edge_sem, halo_send, halo_recv, x_send, x_recv, y_send, y_recv,
    first_x_send, first_x_recv, first_y_send, first_y_recv,
):
    r, c = lax.axis_index("row"), lax.axis_index("col")
    rows, cols = x.shape
    blocks = cols // LANES
    src = wrapped.at[0]

    get_top = pltpu.make_async_copy(src.at[pl.ds(0, 8), :], top, edge_sem.at[0])
    get_corner = pltpu.make_async_copy(
        src.at[pl.ds(rows - 8, 8), pl.ds(cols - LANES, LANES)], corner, edge_sem.at[1]
    )
    get_blocks = [
        pltpu.make_async_copy(
            src.at[:, pl.ds(LANES * j, LANES)], x.at[:, pl.ds(LANES * j, LANES)], in_sem.at[j]
        )
        for j in range(blocks)
    ]
    get_blocks[0].start()
    get_top.start()
    get_corner.start()
    for j in [blocks - 1] + list(range(1, blocks - 1)):
        get_blocks[j].start()

    barrier = pltpu.get_barrier_semaphore()
    for d in range(1, n_row):
        pl.semaphore_signal(
            barrier, inc=1, device_id={"row": lax.rem(r + d, n_row)}, device_id_type=MESH
        )
    for d in range(1, n_col):
        pl.semaphore_signal(
            barrier, inc=1, device_id={"col": lax.rem(c + d, n_col)}, device_id_type=MESH
        )

    get_blocks[0].wait()
    for s in range(8):
        turned = x[pl.ds(LANES * s, LANES), pl.ds(0, LANES)].T
        own_col[pl.ds(s, 1), :] = turned[0:1, :]
    get_top.wait()
    get_corner.wait()
    pl.semaphore_wait(barrier, n_row + n_col - 2)

    def halo(src_ref, dst_ref, k, device):
        return pltpu.make_async_remote_copy(
            src_ref=src_ref, dst_ref=dst_ref, send_sem=halo_send.at[k], recv_sem=halo_recv.at[k],
            device_id=device, device_id_type=MESH,
        )

    halos = [
        halo(own_col, beyond_col, 0, {"col": lax.rem(c + n_col - 1, n_col)}),
        halo(top.at[pl.ds(0, 1), :], below.at[pl.ds(0, 1), :], 1, {"row": lax.rem(r + n_row - 1, n_row)}),
        halo(corner, corner_up, 2, {"row": lax.rem(r + 1, n_row)}),
        halo(corner, corner_left, 3, {"col": lax.rem(c + 1, n_col)}),
    ]
    for copy in halos:
        copy.start()

    get_blocks[blocks - 1].wait()
    for s in range(8):
        turned = x[pl.ds(LANES * s, LANES), pl.ds(cols - LANES, LANES)].T
        own_last[pl.ds(s, 1), :] = turned[LANES - 2 : LANES - 1, :]
        own_last[pl.ds(8 + s, 1), :] = turned[LANES - 1 : LANES, :]
    for j in range(1, blocks - 1):
        get_blocks[j].wait()

    def strip(k, carry):
        at = pl.ds(pl.multiple_of(k * STRIP, STRIP), STRIP)
        here = x[at, :]
        n = turns(here - pltpu.roll(here, 1, 1))
        lane = lax.broadcasted_iota(jnp.int32, (STRIP, LANES), 1)
        parts = [n[:, LANES * j : LANES * (j + 1)] for j in range(blocks)]
        parts[0] = jnp.where(lane == 0, 0.0, parts[0])
        for j in range(blocks):
            m[at, pl.ds(LANES * j, LANES)] = parts[j].astype(jnp.bfloat16)
        while len(parts) > 1:
            parts = [a + b for a, b in zip(parts[::2], parts[1::2])]
        acc[at, :] = parts[0].astype(jnp.bfloat16)
        return carry

    lax.fori_loop(0, rows // STRIP, strip, 0, unroll=2)

    sub, lane = positions((8, LANES))
    flat_totals = lax.dot_general(
        jnp.ones((8, LANES), jnp.bfloat16), acc[...], (((1,), (1,)), ((), ())),
        preferred_element_type=jnp.float32,
    )
    row_totals = jnp.zeros((8, LANES), jnp.float32)
    for s in range(8):
        row_totals = jnp.where(sub == s, flat_totals[:, LANES * s : LANES * (s + 1)], row_totals)

    def row_line(ref, i):
        return jnp.concatenate([ref[i : i + 1, LANES * s : LANES * (s + 1)] for s in range(8)], axis=0)

    col0 = own_col[...]
    col_in, col_out = own_last[0:8, :], own_last[8:16, :]
    row_in, row_out = row_line(x, rows - 2), row_line(x, rows - 1)

    for copy in halos:
        copy.wait_recv()
    right_col = beyond_col[...]
    below_row = row_line(below, 0)

    weight_x = edge_weight(
        col_in, col_out, corner_up[7:8, LANES - 2 : LANES - 1], corner_up[7:8, LANES - 1 : LANES], r == 0
    )
    weight_y = edge_weight(
        row_in, row_out, corner_left[6:7, LANES - 1 : LANES], corner_left[7:8, LANES - 1 : LANES], c == 0
    )
    stack = jnp.concatenate([line_turns(v) for v in (right_col, col0, below_row, row_out)], axis=0)
    sub32, _ = positions(stack.shape)
    sub32 = lax.rem(sub32, 8)
    carry = jnp.where(sub32 >= 1, pltpu.roll(stack, 1, 0), 0.0)
    for step in (1, 2, 4):
        carry = carry + jnp.where(sub32 >= step, pltpu.roll(carry, step, 0), 0.0)
    ka, kb = positions((2 * LANES, LANES))
    prefix = jnp.dot(
        jnp.concatenate([stack, carry], axis=1).astype(jnp.bfloat16),
        ((ka <= kb) | (ka >= LANES)).astype(jnp.float32).astype(jnp.bfloat16),
        preferred_element_type=jnp.float32,
    )
    down = prefix[8:16]
    miss_x = prefix[0:8] - down - row_totals - turns(right_col - col_out)
    miss_y = prefix[16:24] - prefix[24:32] - down[7:8, LANES - 1 : LANES] - turns(below_row - row_out)
    mean_x = total(weight_x * miss_x) / total(weight_x) + col_steps[0, 0, 0].astype(jnp.float32)
    mean_y = total(weight_y * miss_y) / total(weight_y) + row_steps[0, 0, 0].astype(jnp.float32)
    jump_x[...] = jnp.broadcast_to(mean_x, (8, LANES))
    jump_y[...] = jnp.broadcast_to(mean_y, (8, LANES))

    def to_row(d):
        return pltpu.make_async_remote_copy(
            src_ref=jump_y.at[pl.ds(0, 1), :], dst_ref=seen_y.at[pl.ds(r, 1), :],
            send_sem=y_send.at[d - 1], recv_sem=y_recv.at[d - 1],
            device_id={"row": lax.rem(r + d, n_row)}, device_id_type=MESH,
        )

    def to_col(d):
        return pltpu.make_async_remote_copy(
            src_ref=jump_x.at[pl.ds(0, 1), :], dst_ref=seen_x.at[pl.ds(c, 1), :],
            send_sem=x_send.at[d - 1], recv_sem=x_recv.at[d - 1],
            device_id={"col": lax.rem(c + d, n_col)}, device_id_type=MESH,
        )

    first = [to_row(d) for d in range(1, n_row)] + [to_col(d) for d in range(1, n_col)]
    for copy in first:
        copy.start()

    for s in range(8):
        mcol[pl.ds(LANES * s, LANES), :] = jnp.broadcast_to(down[s : s + 1, :], (LANES, LANES)).T
    ta, tb = positions(tri.shape)
    tri[...] = (ta - (rows - 256) <= tb).astype(jnp.float32).astype(jnp.bfloat16)

    def finish(k, carry):
        at = pl.ds(pl.multiple_of(k * 256, 256), 256)
        base = mcol[at, :]
        base = jnp.concatenate([base, base], axis=1)
        for j in range(cols // 256):
            width = 256 * (j + 1)
            counted = jnp.dot(
                m[at, pl.ds(0, width)], tri[pl.ds(rows - width, width), :],
                preferred_element_type=jnp.float32,
            )
            here = pl.ds(256 * j, 256)
            pre[at, here] = x[at, here] * PER_CYCLE - counted - base
        return carry

    lax.fori_loop(0, rows // 256, finish, 0)

    for copy in first:
        copy.wait_recv()
    seen = lax.broadcasted_iota(jnp.int32, (n_col, LANES), 0)
    across = jnp.sum(jnp.where(seen < c, seen_x[...], 0.0), axis=0, keepdims=True)
    seen = lax.broadcasted_iota(jnp.int32, (n_row, LANES), 0)
    downs = jnp.sum(jnp.where(seen < r, seen_y[...], 0.0), axis=0, keepdims=True)
    sum_x[...] = jnp.broadcast_to(across, (8, LANES))
    sum_y[...] = jnp.broadcast_to(downs, (8, LANES))

    def first_row(t):
        return pltpu.make_async_remote_copy(
            src_ref=sum_x.at[pl.ds(0, 1), :], dst_ref=first_x.at[pl.ds(0, 1), :],
            send_sem=first_x_send.at[t - 1], recv_sem=first_x_recv.at[0],
            device_id={"row": t}, device_id_type=MESH,
        )

    def first_col(t):
        return pltpu.make_async_remote_copy(
            src_ref=sum_y.at[pl.ds(0, 1), :], dst_ref=first_y.at[pl.ds(0, 1), :],
            send_sem=first_y_send.at[t - 1], recv_sem=first_y_recv.at[0],
            device_id={"col": t}, device_id_type=MESH,
        )

    @pl.when(r == 0)
    def _():
        for t in range(1, n_row):
            first_row(t).start()

    @pl.when(c == 0)
    def _():
        for t in range(1, n_col):
            first_col(t).start()

    @pl.when(r != 0)
    def _():
        first_row(1).wait_recv()

    @pl.when(c != 0)
    def _():
        first_col(1).wait_recv()

    across_top = jnp.where(r == 0, across, first_x[0:1, :])
    downs_left = jnp.where(c == 0, downs, first_y[0:1, :])

    mine = top_tile = left_tile = origin = jnp.zeros((1, LANES), jnp.float32)
    for sweep in range(ITERS):
        prefix_across = across + left_tile - mine
        prefix_across_top = across_top + origin - top_tile
        prefix_down = downs + top_tile - mine
        prefix_down_left = downs_left + origin - left_tile
        mine = mine + 0.5 * (prefix_across + prefix_across_top + prefix_down + prefix_down_left)
        top_tile = top_tile + 0.5 * (prefix_across_top + prefix_across_top)
        left_tile = left_tile + 0.5 * (prefix_down_left + prefix_down_left)
    offset[...] = jnp.broadcast_to(mine, (8, LANES))

    for copy in halos + first:
        copy.wait_send()

    @pl.when(r == 0)
    def _():
        for t in range(1, n_row):
            first_row(t).wait_send()

    @pl.when(c == 0)
    def _():
        for t in range(1, n_col):
            first_col(t).wait_send()


def on_device(n_row, n_col, wrapped, col_steps, row_steps):
    _, rows, cols = wrapped.shape
    f32 = jnp.float32
    line = pltpu.VMEM((8, LANES), f32)
    dma = pltpu.SemaphoreType.DMA
    in_hbm = pl.BlockSpec(memory_space=pltpu.HBM)
    in_smem = pl.BlockSpec(memory_space=pltpu.SMEM)
    in_vmem = pl.BlockSpec(memory_space=pltpu.VMEM)
    pre, offset = pl.pallas_call(
        functools.partial(kernel, n_row, n_col),
        out_shape=(jax.ShapeDtypeStruct((rows, cols), f32), jax.ShapeDtypeStruct((8, LANES), f32)),
        in_specs=[in_hbm, in_smem, in_smem],
        out_specs=(in_vmem, in_vmem),
        scratch_shapes=[
            pltpu.VMEM((rows, cols), f32),
            pltpu.VMEM((rows, cols), jnp.bfloat16),
            pltpu.VMEM((rows, LANES), jnp.bfloat16),
            pltpu.VMEM((rows, LANES), f32),
            pltpu.VMEM((rows, 256), jnp.bfloat16),
            pltpu.VMEM((8, cols), f32),
            line,
            line,
            pltpu.VMEM((16, LANES), f32),
            line,
            pltpu.VMEM((8, cols), f32),
            line,
            line,
            line,
            line,
            pltpu.VMEM((n_col, LANES), f32),
            pltpu.VMEM((n_row, LANES), f32),
            line,
            line,
            line,
            line,
            dma((cols // LANES,)),
            dma((2,)),
            dma((4,)),
            dma((4,)),
            dma((n_col - 1,)),
            dma((n_col - 1,)),
            dma((n_row - 1,)),
            dma((n_row - 1,)),
            dma((n_row - 1,)),
            dma((1,)),
            dma((n_col - 1,)),
            dma((1,)),
        ],
        compiler_params=pltpu.CompilerParams(
            collective_id=0, has_side_effects=True, vmem_limit_bytes=24 * 1024 * 1024
        ),
    )(pltpu.with_memory_space_constraint(wrapped, pltpu.HBM), col_steps, row_steps)
    return (pre + offset[0:1, 0:1])[None]


def solution(mesh):
    spec = P(None, "row", "col")
    return jax.shard_map(
        functools.partial(on_device, mesh.shape["row"], mesh.shape["col"]),
        mesh=mesh, in_specs=(spec, spec, spec), out_specs=spec, check_vma=False,
    )
```

time: 166 us -> 26.8 us (0.16)
  blocking collectives: 60.9 us -> 0 us
  local copies, waits for them, and re-layouts: 47.6 us -> 0.51 us
  other arithmetic: 34.1 us -> 3.07 us
  Pallas kernels: 0 us -> 21.8 us
  starting transfers between devices: 11.6 us -> 0 us
  matrix products: 5.29 us -> 0 us
  between operations: 5.5 us -> 1.31 us
    all_gather x1 -> x0, blocking collectives: 60.9 us -> none  [gather_turned(): lax.all_gather(both, axis, axis=0, tiled=True)]
    pallas_call x0 -> x1, Pallas kernels: none -> 21.8 us  [on_device(): pl.pallas_call(functools.partial(kernel, n_row, n_col), out_shape=(jax.Sh...]
    concatenate x2 -> x0, local copies, waits for them, and re-layouts: 21.6 us -> none  [with_halo(): jnp.concatenate([jnp.pad(low, around), x, jnp.pad(high, around)], axis=dim)]
    sub x10 -> x0, other arithmetic: 12.7 us -> none  [the longest x4 12.6 us: wrap_diff(): return change - TWO_PI * jnp.floor(change / TWO_PI + 0.5)]
    ppermute x4 -> x0, starting transfers between devices: 11.6 us -> none  [the longest x2 7.49 us: with_halo(): lax.ppermute(last, axis, up)]
    slice x15 -> x1, local copies, waits for them, and re-layouts: 10.9 us -> 0.51 us  [on_device(): return (pre + offset[0:1, 0:1])[None]]
    add x6 -> x0, other arithmetic: 8 us -> none  [the longest x1 2.61 us: mean_jump(): own_edge + crossing - beyond]
    unnamed x5 -> x0, local copies, waits for them, and re-layouts: 7.52 us -> none
  transfers between devices with their start and end apart: 4 -> 0, of which waited for: 0 -> 0; matrix products, arithmetic and copies ran while one was open for 9% -> 0% of each run, Pallas kernels for 0% -> 0%
where the time goes in v1:
time: 26.8 us; the launch traced here: 26.6 us
  Pallas kernels  21.8 us (81%)
  other arithmetic  3.07 us (11%)
  between operations  1.31 us (5%)
  local copies, waits for them, and re-layouts  0.51 us (2%)
    pallas_call x1, Pallas kernels, on_device(): pl.pallas_call(functools.partial(kernel, n_row, n_col), out_shape=(jax.Sh...  21.8 us
    broadcast_in_dim x1, other arithmetic, on_device(): return (pre + offset[0:1, 0:1])[None]  3.07 us

profile of v1, /device:TPU:1, one launch (start us, length us, event | category | flops | bytes accessed | tf_op | source)
XLA Modules:
  0.0 26.6 jit_solution(10569769753066790815)
XLA Ops:
  1.3 21.8 %shard_map.37 = (f32[1024,1024]{1,0:T(8,128)S(1)}, f32[8,128]{1,0:T(8,128)S(1)}) custom-call(f32[1,1024,1024]{2,1,0:T(8,128)} %wrapped.1, s32[1,1,1]{2,1,0:T(1,128)S(6)} %copy.4.col_steps, s32[1,1,1]{2,1,0:T(1,128)S(6)} %copy.5.row_steps), custom_call_target="tpu_custom_call" | custom-call | tf_op jit(solution)/shard_map/pallas_call | solution.py:300
  23.1 0.5 %slice.3 = f32[1,1]{1,0:T(1,128)} slice(f32[8,128]{1,0:T(8,128)S(1)} %get-tuple-element.8), slice={[0:1], [0:1]} | slice | bytes 8 | tf_op jit(solution)/shard_map/slice | solution.py:344
  23.6 3.1 %add_bitcast_fusion = f32[1,1024,1024]{2,1,0:T(8,128)} fusion(f32[1024,1024]{1,0:T(8,128)S(1)} %get-tuple-element.7, f32[]{:T(128)} %bitcast), kind=kLoop, calls=%fused_computation | loop fusion | flops 1048576 | bytes 8388612 | tf_op jit(solution)/shard_map/broadcast_in_dim | solution.py:344

commit v2 on v1

--- a/solution.py
+++ b/solution.py
@@ -12,7 +12,10 @@
 PER_CYCLE = 1.0 / (2.0 * math.pi)
 MESH = pl.DeviceIdType.MESH
 LANES = 128
-STRIP = 32
+STRIP = 16
+UNROLL = 16
+PIECES = 8
+NEAR = 3
 
 
 def turns(change):
@@ -53,7 +56,7 @@
     n_row, n_col, wrapped, col_steps, row_steps, pre, offset,
     x, m, acc, mcol, tri, top, corner, own_col, own_last, beyond_col, below, corner_up, corner_left,
     jump_x, jump_y, seen_x, seen_y, sum_x, sum_y, first_x, first_y,
-    in_sem, edge_sem, halo_send, halo_recv, x_send, x_recv, y_send, y_recv,
+    in_sem, edge_sem, halo_send, halo_recv, ready_x, ready_y, x_send, x_recv, y_send, y_recv,
     first_x_send, first_x_recv, first_y_send, first_y_recv,
 ):
     r, c = lax.axis_index("row"), lax.axis_index("col")
@@ -71,21 +74,32 @@
         )
         for j in range(blocks)
     ]
-    get_blocks[0].start()
     get_top.start()
     get_corner.start()
+    get_blocks[0].start()
     for j in [blocks - 1] + list(range(1, blocks - 1)):
         get_blocks[j].start()
 
     barrier = pltpu.get_barrier_semaphore()
-    for d in range(1, n_row):
-        pl.semaphore_signal(
-            barrier, inc=1, device_id={"row": lax.rem(r + d, n_row)}, device_id_type=MESH
-        )
-    for d in range(1, n_col):
-        pl.semaphore_signal(
-            barrier, inc=1, device_id={"col": lax.rem(c + d, n_col)}, device_id_type=MESH
-        )
+
+    def greet(device):
+        pl.semaphore_signal(barrier, inc=1, device_id=device, device_id_type=MESH)
+
+    @pl.when(c > 0)
+    def _():
+        greet({"col": c - 1})
+
+    @pl.when(r > 0)
+    def _():
+        greet({"row": r - 1})
+
+    @pl.loop(r + 1, n_row)
+    def _(t):
+        greet({"row": t})
+
+    @pl.loop(c + 1, n_col)
+    def _(t):
+        greet({"col": t})
 
     get_blocks[0].wait()
     for s in range(8):
@@ -93,7 +107,8 @@
         own_col[pl.ds(s, 1), :] = turned[0:1, :]
     get_top.wait()
     get_corner.wait()
-    pl.semaphore_wait(barrier, n_row + n_col - 2)
+    has_right, has_below = c < n_col - 1, r < n_row - 1
+    pl.semaphore_wait(barrier, r + c + has_right.astype(jnp.int32) + has_below.astype(jnp.int32))
 
     def halo(src_ref, dst_ref, k, device):
         return pltpu.make_async_remote_copy(
@@ -101,14 +116,29 @@
             device_id=device, device_id_type=MESH,
         )
 
-    halos = [
-        halo(own_col, beyond_col, 0, {"col": lax.rem(c + n_col - 1, n_col)}),
-        halo(top.at[pl.ds(0, 1), :], below.at[pl.ds(0, 1), :], 1, {"row": lax.rem(r + n_row - 1, n_row)}),
-        halo(corner, corner_up, 2, {"row": lax.rem(r + 1, n_row)}),
-        halo(corner, corner_left, 3, {"col": lax.rem(c + 1, n_col)}),
-    ]
-    for copy in halos:
-        copy.start()
+    to_left = halo(own_col, beyond_col, 0, {"col": lax.rem(c + n_col - 1, n_col)})
+    to_above = halo(top.at[pl.ds(0, 1), :], below.at[pl.ds(0, 1), :], 1, {"row": lax.rem(r + n_row - 1, n_row)})
+    to_below = halo(corner, corner_up, 2, {"row": lax.rem(r + 1, n_row)})
+    to_right = halo(corner, corner_left, 3, {"col": lax.rem(c + 1, n_col)})
+    sends = ((c > 0, to_left), (r > 0, to_above), (has_below, to_below), (has_right, to_right))
+    arrivals = ((has_right, to_left), (has_below, to_above), (r > 0, to_below), (c > 0, to_right))
+
+    for holds, copy in sends:
+        @pl.when(holds)
+        def _(copy=copy):
+            copy.start()
+
+    @pl.loop(0, r)
+    def _(k):
+        pl.semaphore_signal(
+            ready_y.at[r], inc=1, device_id={"row": r - 1 - k}, device_id_type=MESH
+        )
+
+    @pl.loop(0, c)
+    def _(k):
+        pl.semaphore_signal(
+            ready_x.at[c], inc=1, device_id={"col": c - 1 - k}, device_id_type=MESH
+        )
 
     get_blocks[blocks - 1].wait()
     for s in range(8):
@@ -118,21 +148,22 @@
     for j in range(1, blocks - 1):
         get_blocks[j].wait()
 
-    def strip(k, carry):
+    @pl.loop(0, rows // STRIP, unroll=UNROLL)
+    def _(k):
         at = pl.ds(pl.multiple_of(k * STRIP, STRIP), STRIP)
-        here = x[at, :]
-        n = turns(here - pltpu.roll(here, 1, 1))
         lane = lax.broadcasted_iota(jnp.int32, (STRIP, LANES), 1)
-        parts = [n[:, LANES * j : LANES * (j + 1)] for j in range(blocks)]
-        parts[0] = jnp.where(lane == 0, 0.0, parts[0])
+        counts, moved = [], None
         for j in range(blocks):
-            m[at, pl.ds(LANES * j, LANES)] = parts[j].astype(jnp.bfloat16)
-        while len(parts) > 1:
-            parts = [a + b for a, b in zip(parts[::2], parts[1::2])]
-        acc[at, :] = parts[0].astype(jnp.bfloat16)
-        return carry
-
-    lax.fori_loop(0, rows // STRIP, strip, 0, unroll=2)
+            here = x[at, pl.ds(LANES * j, LANES)]
+            last, moved = moved, pltpu.roll(here, 1, 1)
+            back = moved if j == 0 else jnp.where(lane == 0, last, moved)
+            n = turns(here - back)
+            n = jnp.where(lane == 0, 0.0, n) if j == 0 else n
+            m[j, at, :] = n.astype(jnp.bfloat16)
+            counts.append(n)
+        while len(counts) > 1:
+            counts = [a + b for a, b in zip(counts[::2], counts[1::2])]
+        acc[at, :] = counts[0].astype(jnp.bfloat16)
 
     sub, lane = positions((8, LANES))
     flat_totals = lax.dot_general(
@@ -150,11 +181,13 @@
     col_in, col_out = own_last[0:8, :], own_last[8:16, :]
     row_in, row_out = row_line(x, rows - 2), row_line(x, rows - 1)
 
-    for copy in halos:
-        copy.wait_recv()
+    for holds, copy in arrivals:
+        @pl.when(holds)
+        def _(copy=copy):
+            copy.wait_recv()
+
     right_col = beyond_col[...]
     below_row = row_line(below, 0)
-
     weight_x = edge_weight(
         col_in, col_out, corner_up[7:8, LANES - 2 : LANES - 1], corner_up[7:8, LANES - 1 : LANES], r == 0
     )
@@ -181,47 +214,71 @@
     jump_x[...] = jnp.broadcast_to(mean_x, (8, LANES))
     jump_y[...] = jnp.broadcast_to(mean_y, (8, LANES))
 
-    def to_row(d):
+    def to_row(t):
         return pltpu.make_async_remote_copy(
             src_ref=jump_y.at[pl.ds(0, 1), :], dst_ref=seen_y.at[pl.ds(r, 1), :],
-            send_sem=y_send.at[d - 1], recv_sem=y_recv.at[d - 1],
-            device_id={"row": lax.rem(r + d, n_row)}, device_id_type=MESH,
-        )
-
-    def to_col(d):
+            send_sem=y_send.at[t], recv_sem=y_recv.at[r],
+            device_id={"row": t}, device_id_type=MESH,
+        )
+
+    def to_col(t):
         return pltpu.make_async_remote_copy(
             src_ref=jump_x.at[pl.ds(0, 1), :], dst_ref=seen_x.at[pl.ds(c, 1), :],
-            send_sem=x_send.at[d - 1], recv_sem=x_recv.at[d - 1],
-            device_id={"col": lax.rem(c + d, n_col)}, device_id_type=MESH,
-        )
-
-    first = [to_row(d) for d in range(1, n_row)] + [to_col(d) for d in range(1, n_col)]
-    for copy in first:
-        copy.start()
+            send_sem=x_send.at[t], recv_sem=x_recv.at[c],
+            device_id={"col": t}, device_id_type=MESH,
+        )
+
+    def send_y(t):
+        pl.semaphore_wait(ready_y.at[t], 1)
+        to_row(t).start()
+
+    def send_x(t):
+        pl.semaphore_wait(ready_x.at[t], 1)
+        to_col(t).start()
+
+    stop_x = jnp.where(c < n_col // 4, n_col // 2, n_col)
+    near_y, near_x = jnp.minimum(r + 1 + NEAR, n_row), jnp.minimum(c + 1 + NEAR, stop_x)
+    pl.loop(r + 1, near_y)(send_y)
+    pl.loop(c + 1, near_x)(send_x)
 
     for s in range(8):
         mcol[pl.ds(LANES * s, LANES), :] = jnp.broadcast_to(down[s : s + 1, :], (LANES, LANES)).T
     ta, tb = positions(tri.shape)
-    tri[...] = (ta - (rows - 256) <= tb).astype(jnp.float32).astype(jnp.bfloat16)
-
-    def finish(k, carry):
+    tri[...] = ((ta <= tb) | (tb >= 2 * LANES)).astype(jnp.float32).astype(jnp.bfloat16)
+
+    @pl.loop(0, rows // 256)
+    def _(k):
         at = pl.ds(pl.multiple_of(k * 256, 256), 256)
         base = mcol[at, :]
-        base = jnp.concatenate([base, base], axis=1)
-        for j in range(cols // 256):
-            width = 256 * (j + 1)
+        for j in range(blocks // 2):
             counted = jnp.dot(
-                m[at, pl.ds(0, width)], tri[pl.ds(rows - width, width), :],
+                jnp.concatenate([m[2 * j, at, :], m[2 * j + 1, at, :]], axis=1), tri[...],
                 preferred_element_type=jnp.float32,
             )
-            here = pl.ds(256 * j, 256)
-            pre[at, here] = x[at, here] * PER_CYCLE - counted - base
-        return carry
-
-    lax.fori_loop(0, rows // 256, finish, 0)
-
-    for copy in first:
-        copy.wait_recv()
+            for h in range(2):
+                here = pl.ds(LANES * (2 * j + h), LANES)
+                pre[at, here] = x[at, here] * PER_CYCLE - counted[:, LANES * h : LANES * (h + 1)] - base
+            base = base + counted[:, 2 * LANES :]
+
+    pl.loop(near_y, n_row)(send_y)
+    pl.loop(near_x, stop_x)(send_x)
+
+    @pl.loop(0, r)
+    def _(k):
+        pltpu.make_async_remote_copy(
+            src_ref=jump_y.at[pl.ds(0, 1), :], dst_ref=seen_y.at[pl.ds(k, 1), :],
+            send_sem=y_send.at[k], recv_sem=y_recv.at[k],
+            device_id={"row": k}, device_id_type=MESH,
+        ).wait_recv()
+
+    @pl.loop(0, c)
+    def _(k):
+        pltpu.make_async_remote_copy(
+            src_ref=jump_x.at[pl.ds(0, 1), :], dst_ref=seen_x.at[pl.ds(k, 1), :],
+            send_sem=x_send.at[k], recv_sem=x_recv.at[k],
+            device_id={"col": k}, device_id_type=MESH,
+        ).wait_recv()
+
     seen = lax.broadcasted_iota(jnp.int32, (n_col, LANES), 0)
     across = jnp.sum(jnp.where(seen < c, seen_x[...], 0.0), axis=0, keepdims=True)
     seen = lax.broadcasted_iota(jnp.int32, (n_row, LANES), 0)
@@ -232,25 +289,35 @@
     def first_row(t):
         return pltpu.make_async_remote_copy(
             src_ref=sum_x.at[pl.ds(0, 1), :], dst_ref=first_x.at[pl.ds(0, 1), :],
-            send_sem=first_x_send.at[t - 1], recv_sem=first_x_recv.at[0],
+            send_sem=first_x_send.at[t], recv_sem=first_x_recv.at[0],
             device_id={"row": t}, device_id_type=MESH,
         )
 
     def first_col(t):
         return pltpu.make_async_remote_copy(
             src_ref=sum_y.at[pl.ds(0, 1), :], dst_ref=first_y.at[pl.ds(0, 1), :],
-            send_sem=first_y_send.at[t - 1], recv_sem=first_y_recv.at[0],
+            send_sem=first_y_send.at[t], recv_sem=first_y_recv.at[0],
             device_id={"col": t}, device_id_type=MESH,
         )
 
     @pl.when(r == 0)
     def _():
-        for t in range(1, n_row):
+        @pl.loop(1, n_row)
+        def _(t):
             first_row(t).start()
 
-    @pl.when(c == 0)
-    def _():
-        for t in range(1, n_col):
+    head_y = jnp.where(c == 0, stop_x, 1)
+
+    @pl.loop(1, head_y)
+    def _(t):
+        first_col(t).start()
+
+    @pl.loop(stop_x, n_col)
+    def _(t):
+        send_x(t)
+
+        @pl.when(c == 0)
+        def _():
             first_col(t).start()
 
     @pl.when(r != 0)
@@ -275,18 +342,43 @@
         left_tile = left_tile + 0.5 * (prefix_down_left + prefix_down_left)
     offset[...] = jnp.broadcast_to(mine, (8, LANES))
 
-    for copy in halos + first:
-        copy.wait_send()
+    for holds, copy in sends:
+        @pl.when(holds)
+        def _(copy=copy):
+            copy.wait_send()
+
+    @pl.loop(r + 1, n_row)
+    def _(t):
+        to_row(t).wait_send()
+
+    @pl.loop(c + 1, n_col)
+    def _(t):
+        to_col(t).wait_send()
 
     @pl.when(r == 0)
     def _():
-        for t in range(1, n_row):
+        @pl.loop(1, n_row)
+        def _(t):
             first_row(t).wait_send()
 
     @pl.when(c == 0)
     def _():
-        for t in range(1, n_col):
+        @pl.loop(1, n_col)
+        def _(t):
             first_col(t).wait_send()
+
+
+def add_offset(pre, offset, out, done, sem):
+    piece = pre.shape[0] // PIECES
+    copies = []
+    for k in range(PIECES):
+        at = pl.ds(k * piece, piece)
+        done[at, :] = pre[at, :] + offset[0:1, 0:1]
+        copy = pltpu.make_async_copy(done.at[at, :], out.at[0, at, :], sem.at[k])
+        copy.start()
+        copies.append(copy)
+    for copy in copies:
+        copy.wait()
 
 
 def on_device(n_row, n_col, wrapped, col_steps, row_steps):
@@ -304,10 +396,10 @@
         out_specs=(in_vmem, in_vmem),
         scratch_shapes=[
             pltpu.VMEM((rows, cols), f32),
-            pltpu.VMEM((rows, cols), jnp.bfloat16),
+            pltpu.VMEM((cols // LANES, rows, LANES), jnp.bfloat16),
             pltpu.VMEM((rows, LANES), jnp.bfloat16),
             pltpu.VMEM((rows, LANES), f32),
-            pltpu.VMEM((rows, 256), jnp.bfloat16),
+            pltpu.VMEM((2 * LANES, 3 * LANES), jnp.bfloat16),
             pltpu.VMEM((8, cols), f32),
             line,
             line,
@@ -328,20 +420,30 @@
             dma((2,)),
             dma((4,)),
             dma((4,)),
-            dma((n_col - 1,)),
-            dma((n_col - 1,)),
-            dma((n_row - 1,)),
-            dma((n_row - 1,)),
-            dma((n_row - 1,)),
+            pltpu.SemaphoreType.REGULAR((n_col,)),
+            pltpu.SemaphoreType.REGULAR((n_row,)),
+            dma((n_col,)),
+            dma((n_col,)),
+            dma((n_row,)),
+            dma((n_row,)),
+            dma((n_row,)),
             dma((1,)),
-            dma((n_col - 1,)),
+            dma((n_col,)),
             dma((1,)),
         ],
         compiler_params=pltpu.CompilerParams(
             collective_id=0, has_side_effects=True, vmem_limit_bytes=24 * 1024 * 1024
         ),
     )(pltpu.with_memory_space_constraint(wrapped, pltpu.HBM), col_steps, row_steps)
-    return (pre + offset[0:1, 0:1])[None]
+    out = pl.pallas_call(
+        add_offset,
+        out_shape=jax.ShapeDtypeStruct((1, rows, cols), f32),
+        in_specs=[in_vmem, in_vmem],
+        out_specs=in_hbm,
+        scratch_shapes=[pltpu.VMEM((rows, cols), f32), dma((PIECES,))],
+        compiler_params=pltpu.CompilerParams(vmem_limit_bytes=8 * 1024 * 1024),
+    )(pre, offset)
+    return out
 
 
 def solution(mesh):

time: 26.8 us -> 20.5 us (0.76)
  the two profiles are of different devices: /device:TPU:1 before, /device:TPU:38 now
where the time goes in v2:
time: 20.5 us; the launch traced here: 20.4 us
  Pallas kernels  19.1 us (93%)
  between operations  1.3 us (6%)
    pallas_call x1, Pallas kernels, on_device(): pl.pallas_call(functools.partial(kernel, n_row, n_col), out_shape=(jax.Sh...  16.9 us
    pallas_call x1, Pallas kernels, on_device(): pl.pallas_call(add_offset, out_shape=jax.ShapeDtypeStruct((1, rows, cols)...  2.14 us

profile of v2, /device:TPU:38, one launch (start us, length us, event | category | flops | bytes accessed | tf_op | source)
XLA Modules:
  0.0 20.4 jit_solution(13196701801345911750)
XLA Ops:
  1.3 16.9 %shard_map.37 = (f32[1024,1024]{1,0:T(8,128)S(1)}, f32[8,128]{1,0:T(8,128)S(1)}) custom-call(f32[1,1024,1024]{2,1,0:T(8,128)} %wrapped.1, s32[1,1,1]{2,1,0:T(1,128)S(6)} %copy.4.col_steps, s32[1,1,1]{2,1,0:T(1,128)S(6)} %copy.5.row_steps), custom_call_target="tpu_custom_call" | custom-call | tf_op jit(solution)/shard_map/pallas_call | solution.py:392
  18.2 2.1 %shard_map.38 = f32[1,1024,1024]{2,1,0:T(8,128)} custom-call(f32[1024,1024]{1,0:T(8,128)S(1)} %get-tuple-element.7.pre, f32[8,128]{1,0:T(8,128)S(1)} %get-tuple-element.8.offset), custom_call_target="tpu_custom_call" | custom-call | tf_op jit(solution)/shard_map/pallas_call | solution.py:438

commit v3 on v2

v3 whole, which is shorter than its diff:
```python
import functools
import math

import jax
import jax.numpy as jnp
from jax import lax
from jax.experimental import pallas as pl
from jax.experimental.pallas import tpu as pltpu
from jax.sharding import PartitionSpec as P

ITERS = 2
PER_CYCLE = 1.0 / (2.0 * math.pi)
MESH = pl.DeviceIdType.MESH
LANES = 128
STRIP = 16
PARTS = (256, 256, 256, 256)
MEET = 2
PIECES = 8
NEAR = 3


def turns(change):
    return jnp.floor(change * PER_CYCLE + 0.5)


def positions(shape):
    return lax.broadcasted_iota(jnp.int32, shape, 0), lax.broadcasted_iota(jnp.int32, shape, 1)


def before(line, first):
    sub, lane = positions(line.shape)
    along = pltpu.roll(line, 1, 1)
    moved = jnp.where(lane == 0, pltpu.roll(along, 1, 0), along)
    return jnp.where((lane == 0) & (sub == 0), first, moved)


def line_turns(line):
    return turns(line - before(line, line))


def edge_weight(inner, outer, inner_first, outer_first, no_first):
    sub, lane = positions(inner.shape)
    cross = turns(outer - inner)
    cross_before = before(cross, turns(outer_first - inner_first))
    along_inner = turns(inner - before(inner, inner_first))
    along_outer = turns(outer - before(outer, outer_first))
    charge = jnp.abs(cross_before - cross + along_outer - along_inner)
    charge = jnp.where((lane == 0) & (sub == 0) & no_first, 0.0, charge)
    return 1.0 / (1.0 + charge)


def total(x):
    return jnp.sum(jnp.sum(x, axis=1, keepdims=True), axis=0, keepdims=True)


def running_turns(lines):
    stack = jnp.concatenate([line_turns(v) for v in lines], axis=0)
    sub, _ = positions(stack.shape)
    sub = lax.rem(sub, 8)
    carry = jnp.where(sub >= 1, pltpu.roll(stack, 1, 0), 0.0)
    for step in (1, 2, 4):
        carry = carry + jnp.where(sub >= step, pltpu.roll(carry, step, 0), 0.0)
    ka, kb = positions((2 * LANES, LANES))
    prefix = jnp.dot(
        jnp.concatenate([stack, carry], axis=1).astype(jnp.bfloat16),
        ((ka <= kb) | (ka >= LANES)).astype(jnp.float32).astype(jnp.bfloat16),
        preferred_element_type=jnp.float32,
    )
    return [prefix[8 * k : 8 * k + 8] for k in range(len(lines))]


def row_line(ref, i):
    return jnp.concatenate([ref[i : i + 1, LANES * s : LANES * (s + 1)] for s in range(8)], axis=0)


def kernel(
    n_row, n_col, wrapped, col_steps, row_steps, pre, offset,
    x, m, acc, mcol, tri, own_col, bottom, edge_x, edge_y, left, above, corner,
    jump_x, jump_y, seen_x, seen_y, first_x, first_y,
    in_sem, edge_sem, halo_send, halo_recv, ready_x, ready_y, x_send, x_recv, y_send, y_recv, first_recv,
):
    r, c = lax.axis_index("row"), lax.axis_index("col")
    rows, cols = x.shape
    blocks = cols // LANES
    src = wrapped.at[0]

    get_bottom = pltpu.make_async_copy(src.at[pl.ds(rows - 8, 8), :], edge_y, edge_sem.at[0])
    get_corner = pltpu.make_async_copy(
        src.at[pl.ds(rows - 8, 8), pl.ds(cols - LANES, LANES)], bottom, edge_sem.at[1]
    )
    get_parts = [
        pltpu.make_async_copy(
            src.at[pl.ds(sum(PARTS[:k]), part), :], x.at[pl.ds(sum(PARTS[:k]), part), :], in_sem.at[k]
        )
        for k, part in enumerate(PARTS)
    ]
    for copy in get_parts[:1] + [get_bottom, get_corner] + get_parts[1:]:
        copy.start()

    barrier = pltpu.get_barrier_semaphore()

    def greet(device):
        pl.semaphore_signal(barrier, inc=1, device_id=device, device_id_type=MESH)

    @pl.when(c > 0)
    def _():
        greet({"col": c - 1})

    @pl.when(r > 0)
    def _():
        greet({"row": r - 1})

    @pl.when((r > 0) & (c > 0))
    def _():
        greet({"row": r - 1, "col": c - 1})

    @pl.loop(r + 1, n_row)
    def _(t):
        greet({"row": t})

    @pl.loop(c + 1, n_col)
    def _(t):
        greet({"col": t})

    has_right, has_below = c < n_col - 1, r < n_row - 1
    touching = has_right.astype(jnp.int32) + has_below.astype(jnp.int32)
    touching = touching + (has_right & has_below).astype(jnp.int32)

    def meet():
        pl.semaphore_wait(barrier, r + c + touching)

        @pl.loop(0, r)
        def _(k):
            pl.semaphore_signal(
                ready_y.at[r], inc=1, device_id={"row": r - 1 - k}, device_id_type=MESH
            )

        @pl.loop(0, c)
        def _(k):
            pl.semaphore_signal(
                ready_x.at[c], inc=1, device_id={"col": c - 1 - k}, device_id_type=MESH
            )

    first = 0
    for k, part in enumerate(PARTS):
        if k == MEET:
            meet()
        get_parts[k].wait()
        for s in range(first // LANES, (first + part) // LANES):
            at = pl.ds(LANES * s, LANES)
            own_col[pl.ds(s, 1), :] = x[at, pl.ds(0, LANES)].T[0:1, :]
            turned = x[at, pl.ds(cols - LANES, LANES)].T
            edge_x[pl.ds(s, 1), :] = turned[LANES - 2 : LANES - 1, :]
            edge_x[pl.ds(8 + s, 1), :] = turned[LANES - 1 : LANES, :]
        for q in range(first // STRIP, (first + part) // STRIP):
            at = pl.ds(STRIP * q, STRIP)
            lane = lax.broadcasted_iota(jnp.int32, (STRIP, LANES), 1)
            counts, moved = [], None
            for j in range(blocks):
                here = x[at, pl.ds(LANES * j, LANES)]
                last, moved = moved, pltpu.roll(here, 1, 1)
                back = moved if j == 0 else jnp.where(lane == 0, last, moved)
                n = turns(here - back)
                n = jnp.where(lane == 0, 0.0, n) if j == 0 else n
                m[j, at, :] = n.astype(jnp.bfloat16)
                counts.append(n)
            while len(counts) > 1:
                counts = [a + b for a, b in zip(counts[::2], counts[1::2])]
            acc[at, :] = counts[0].astype(jnp.bfloat16)
        first += part

    sub, lane = positions((8, LANES))
    flat_totals = lax.dot_general(
        jnp.ones((8, LANES), jnp.bfloat16), acc[...], (((1,), (1,)), ((), ())),
        preferred_element_type=jnp.float32,
    )
    row_totals = jnp.zeros((8, LANES), jnp.float32)
    for s in range(8):
        row_totals = jnp.where(sub == s, flat_totals[:, LANES * s : LANES * (s + 1)], row_totals)
    (down,) = running_turns([own_col[...]])
    edge_x[16:24, :] = down + row_totals - col_steps[0, 0, 0].astype(jnp.float32)
    get_bottom.wait()
    get_corner.wait()
    down_total = down[7:8, LANES - 1 : LANES] - row_steps[0, 0, 0].astype(jnp.float32)
    for s in range(8):
        edge_y[5:6, LANES * s : LANES * (s + 1)] = jnp.broadcast_to(down_total, (1, LANES))

    def halo(src_ref, dst_ref, k, device):
        return pltpu.make_async_remote_copy(
            src_ref=src_ref, dst_ref=dst_ref, send_sem=halo_send.at[k], recv_sem=halo_recv.at[k],
            device_id=device, device_id_type=MESH,
        )

    next_row, next_col = lax.rem(r + 1, n_row), lax.rem(c + 1, n_col)
    to_right = halo(edge_x, left, 0, {"col": next_col})
    to_below = halo(edge_y.at[pl.ds(5, 3), :], above.at[pl.ds(5, 3), :], 1, {"row": next_row})
    to_both = halo(bottom, corner, 2, {"row": next_row, "col": next_col})
    sends = ((has_below, to_below), (has_right, to_right), (has_right & has_below, to_both))
    arrivals = ((r > 0, to_below), (c > 0, to_right), ((r > 0) & (c > 0), to_both))

    for holds, copy in sends:
        @pl.when(holds)
        def _(copy=copy):
            copy.start()

    for s in range(8):
        mcol[pl.ds(LANES * s, LANES), :] = jnp.broadcast_to(down[s : s + 1, :], (LANES, LANES)).T
    ta, tb = positions(tri.shape)
    tri[...] = ((ta <= tb) | (tb >= 2 * LANES)).astype(jnp.float32).astype(jnp.bfloat16)

    @pl.loop(0, rows // 256)
    def _(k):
        at = pl.ds(pl.multiple_of(k * 256, 256), 256)
        base = mcol[at, :]
        for j in range(blocks // 2):
            counted = jnp.dot(
                jnp.concatenate([m[2 * j, at, :], m[2 * j + 1, at, :]], axis=1), tri[...],
                preferred_element_type=jnp.float32,
            )
            for h in range(2):
                here = pl.ds(LANES * (2 * j + h), LANES)
                pre[at, here] = x[at, here] * PER_CYCLE - counted[:, LANES * h : LANES * (h + 1)] - base
            base = base + counted[:, 2 * LANES :]

    for holds, copy in arrivals:
        @pl.when(holds)
        def _(copy=copy):
            copy.wait_recv()

    col0, row0 = own_col[...], row_line(x, 0)
    col_in, col_out = left[0:8, :], left[8:16, :]
    row_in, row_out = row_line(above, 6), row_line(above, 7)
    weight_x = edge_weight(
        col_in, col_out, corner[7:8, LANES - 2 : LANES - 1], corner[7:8, LANES - 1 : LANES], r == 0
    )
    weight_y = edge_weight(
        row_in, row_out, corner[6:7, LANES - 1 : LANES], corner[7:8, LANES - 1 : LANES], c == 0
    )
    along, along_above = running_turns([row0, row_out])
    miss_x = down - left[16:24, :] - turns(col0 - col_out)
    miss_y = along - along_above - above[5:6, 0:LANES] - turns(row0 - row_out)
    mean_x = total(weight_x * miss_x) / total(weight_x)
    mean_y = total(weight_y * miss_y) / total(weight_y)
    jump_x[...] = jnp.broadcast_to(jnp.where(c == 0, 0.0, mean_x), (8, LANES))
    jump_y[...] = jnp.broadcast_to(jnp.where(r == 0, 0.0, mean_y), (8, LANES))

    def to_row(t):
        return pltpu.make_async_remote_copy(
            src_ref=jump_y.at[pl.ds(0, 1), :], dst_ref=seen_y.at[pl.ds(r, 1), :],
            send_sem=y_send.at[t], recv_sem=y_recv.at[r],
            device_id={"row": t}, device_id_type=MESH,
        )

    def to_col(t):
        return pltpu.make_async_remote_copy(
            src_ref=jump_x.at[pl.ds(0, 1), :], dst_ref=seen_x.at[pl.ds(c, 1), :],
            send_sem=x_send.at[t], recv_sem=x_recv.at[c],
            device_id={"col": t}, device_id_type=MESH,
        )

    def from_row(k):
        return pltpu.make_async_remote_copy(
            src_ref=jump_y.at[pl.ds(0, 1), :], dst_ref=seen_y.at[pl.ds(k, 1), :],
            send_sem=y_send.at[k], recv_sem=y_recv.at[k],
            device_id={"row": k}, device_id_type=MESH,
        )

    def from_col(k):
        return pltpu.make_async_remote_copy(
            src_ref=jump_x.at[pl.ds(0, 1), :], dst_ref=seen_x.at[pl.ds(k, 1), :],
            send_sem=x_send.at[k], recv_sem=x_recv.at[k],
            device_id={"col": k}, device_id_type=MESH,
        )

    def first_row(t):
        return pltpu.make_async_remote_copy(
            src_ref=jump_y.at[pl.ds(0, 1), :], dst_ref=first_y.at[pl.ds(0, 1), :],
            send_sem=y_send.at[t], recv_sem=first_recv.at[0],
            device_id={"row": t}, device_id_type=MESH,
        )

    def first_col(t):
        return pltpu.make_async_remote_copy(
            src_ref=jump_x.at[pl.ds(0, 1), :], dst_ref=first_x.at[pl.ds(0, 1), :],
            send_sem=x_send.at[t], recv_sem=first_recv.at[1],
            device_id={"col": t}, device_id_type=MESH,
        )

    def send_y(t):
        pl.semaphore_wait(ready_y.at[t], 1)
        to_row(t).start()

    def send_x(t):
        pl.semaphore_wait(ready_x.at[t], 1)
        to_col(t).start()

    stop_x = jnp.where(c < n_col // 4, n_col // 2, n_col)
    start_y, start_x = jnp.where(r == 0, n_row, r + 1), jnp.where(c == 0, stop_x, c + 1)
    near_y, near_x = jnp.minimum(start_y + NEAR, n_row), jnp.minimum(start_x + NEAR, stop_x)
    pl.loop(start_y, near_y)(send_y)
    pl.loop(start_x, near_x)(send_x)
    pl.loop(near_y, n_row)(send_y)
    pl.loop(near_x, stop_x)(send_x)

    @pl.loop(1, r)
    def _(k):
        from_row(k).wait_recv()

    @pl.loop(1, c)
    def _(k):
        from_col(k).wait_recv()

    seen = lax.broadcasted_iota(jnp.int32, (n_col, LANES), 0)
    across = jnp.sum(jnp.where((seen > 0) & (seen < c), seen_x[...], 0.0), axis=0, keepdims=True) + jump_x[0:1, :]
    seen = lax.broadcasted_iota(jnp.int32, (n_row, LANES), 0)
    downs = jnp.sum(jnp.where((seen > 0) & (seen < r), seen_y[...], 0.0), axis=0, keepdims=True) + jump_y[0:1, :]

    @pl.when(r == 0)
    def _():
        jump_y[...] = jnp.broadcast_to(across, (8, LANES))

        @pl.loop(1, n_row)
        def _(t):
            pl.semaphore_wait(ready_y.at[t], 1)
            first_row(t).start()

    @pl.when(c == 0)
    def _():
        jump_x[...] = jnp.broadcast_to(downs, (8, LANES))

        @pl.loop(1, n_col)
        def _(t):
            pl.semaphore_wait(ready_x.at[t], 1)
            first_col(t).start()

    @pl.when(c > 0)
    def _():
        pl.loop(stop_x, n_col)(send_x)

    @pl.when(r > 0)
    def _():
        first_row(0).wait_recv()

    @pl.when(c > 0)
    def _():
        first_col(0).wait_recv()

    across_top = jnp.where(r == 0, across, first_y[0:1, :])
    downs_left = jnp.where(c == 0, downs, first_x[0:1, :])

    mine = top_tile = left_tile = origin = jnp.zeros((1, LANES), jnp.float32)
    for sweep in range(ITERS):
        prefix_across = across + left_tile - mine
        prefix_across_top = across_top + origin - top_tile
        prefix_down = downs + top_tile - mine
        prefix_down_left = downs_left + origin - left_tile
        mine = mine + 0.5 * (prefix_across + prefix_across_top + prefix_down + prefix_down_left)
        top_tile = top_tile + 0.5 * (prefix_across_top + prefix_across_top)
        left_tile = left_tile + 0.5 * (prefix_down_left + prefix_down_left)
    offset[...] = jnp.broadcast_to(mine, (8, LANES))

    for holds, copy in sends:
        @pl.when(holds)
        def _(copy=copy):
            copy.wait_send()

    @pl.loop(r + 1, n_row)
    def _(t):
        to_row(t).wait_send()

    @pl.loop(c + 1, n_col)
    def _(t):
        to_col(t).wait_send()


def add_offset(pre, offset, out, done, sem):
    piece = pre.shape[0] // PIECES
    copies = []
    for k in range(PIECES):
        at = pl.ds(k * piece, piece)
        done[at, :] = pre[at, :] + offset[0:1, 0:1]
        copy = pltpu.make_async_copy(done.at[at, :], out.at[0, at, :], sem.at[k])
        copy.start()
        copies.append(copy)
    for copy in copies:
        copy.wait()


def on_device(n_row, n_col, wrapped, col_steps, row_steps):
    _, rows, cols = wrapped.shape
    f32 = jnp.float32
    line = pltpu.VMEM((8, LANES), f32)
    dma = pltpu.SemaphoreType.DMA
    in_hbm = pl.BlockSpec(memory_space=pltpu.HBM)
    in_smem = pl.BlockSpec(memory_space=pltpu.SMEM)
    in_vmem = pl.BlockSpec(memory_space=pltpu.VMEM)
    pre, offset = pl.pallas_call(
        functools.partial(kernel, n_row, n_col),
        out_shape=(jax.ShapeDtypeStruct((rows, cols), f32), jax.ShapeDtypeStruct((8, LANES), f32)),
        in_specs=[in_hbm, in_smem, in_smem],
        out_specs=(in_vmem, in_vmem),
        scratch_shapes=[
            pltpu.VMEM((rows, cols), f32),
            pltpu.VMEM((cols // LANES, rows, LANES), jnp.bfloat16),
            pltpu.VMEM((rows, LANES), jnp.bfloat16),
            pltpu.VMEM((rows, LANES), f32),
            pltpu.VMEM((2 * LANES, 3 * LANES), jnp.bfloat16),
            line,
            line,
            pltpu.VMEM((24, LANES), f32),
            pltpu.VMEM((8, cols), f32),
            pltpu.VMEM((24, LANES), f32),
            pltpu.VMEM((8, cols), f32),
            line,
            line,
            line,
            pltpu.VMEM((n_col, LANES), f32),
            pltpu.VMEM((n_row, LANES), f32),
            line,
            line,
            dma((len(PARTS),)),
            dma((2,)),
            dma((3,)),
            dma((3,)),
            pltpu.SemaphoreType.REGULAR((n_col,)),
            pltpu.SemaphoreType.REGULAR((n_row,)),
            dma((n_col,)),
            dma((n_col,)),
            dma((n_row,)),
            dma((n_row,)),
            dma((2,)),
        ],
        compiler_params=pltpu.CompilerParams(
            collective_id=0, has_side_effects=True, vmem_limit_bytes=24 * 1024 * 1024
        ),
    )(pltpu.with_memory_space_constraint(wrapped, pltpu.HBM), col_steps, row_steps)
    out = pl.pallas_call(
        add_offset,
        out_shape=jax.ShapeDtypeStruct((1, rows, cols), f32),
        in_specs=[in_vmem, in_vmem],
        out_specs=in_hbm,
        scratch_shapes=[pltpu.VMEM((rows, cols), f32), dma((PIECES,))],
        compiler_params=pltpu.CompilerParams(vmem_limit_bytes=8 * 1024 * 1024),
    )(pre, offset)
    return out


def solution(mesh):
    spec = P(None, "row", "col")
    return jax.shard_map(
        functools.partial(on_device, mesh.shape["row"], mesh.shape["col"]),
        mesh=mesh, in_specs=(spec, spec, spec), out_specs=spec, check_vma=False,
    )
```

time: 20.5 us -> 18.1 us (0.88)
  Pallas kernels: 19.1 us -> 16.7 us
    pallas_call x1, Pallas kernels: 16.9 us -> 14.6 us  [on_device(): pl.pallas_call(functools.partial(kernel, n_row, n_col), out_shape=(jax.Sh...]
where the time goes in v3:
time: 18.1 us; the launch traced here: 18 us
  Pallas kernels  16.7 us (92%)
  between operations  1.3 us (7%)
    pallas_call x1, Pallas kernels, on_device(): pl.pallas_call(functools.partial(kernel, n_row, n_col), out_shape=(jax.Sh...  14.6 us
    pallas_call x1, Pallas kernels, on_device(): pl.pallas_call(add_offset, out_shape=jax.ShapeDtypeStruct((1, rows, cols)...  2.14 us

profile of v3, /device:TPU:38, one launch (start us, length us, event | category | flops | bytes accessed | tf_op | source)
XLA Modules:
  0.0 18.0 jit_solution(12469721426110428433)
XLA Ops:
  1.3 14.6 %shard_map.37 = (f32[1024,1024]{1,0:T(8,128)S(1)}, f32[8,128]{1,0:T(8,128)S(1)}) custom-call(f32[1,1024,1024]{2,1,0:T(8,128)} %wrapped.1, s32[1,1,1]{2,1,0:T(1,128)S(6)} %copy.4.col_steps, s32[1,1,1]{2,1,0:T(1,128)S(6)} %copy.5.row_steps), custom_call_target="tpu_custom_call" | custom-call | tf_op jit(solution)/shard_map/pallas_call | solution.py:397
  15.9 2.1 %shard_map.38 = f32[1,1024,1024]{2,1,0:T(8,128)} custom-call(f32[1024,1024]{1,0:T(8,128)S(1)} %get-tuple-element.7.pre, f32[8,128]{1,0:T(8,128)S(1)} %get-tuple-element.8.offset), custom_call_target="tpu_custom_call" | custom-call | tf_op jit(solution)/shard_map/pallas_call | solution.py:437

commit v4 on v3

--- a/solution.py
+++ b/solution.py
@@ -17,6 +17,7 @@
 MEET = 2
 PIECES = 8
 NEAR = 3
+SIDE = 4
 
 
 def turns(change):
@@ -73,9 +74,16 @@
     return jnp.concatenate([ref[i : i + 1, LANES * s : LANES * (s + 1)] for s in range(8)], axis=0)
 
 
+def far_side(low, high):
+    def level(t):
+        return jnp.minimum(lax.div(t, SIDE), SIDE // 2) + jnp.minimum(lax.rem(t, SIDE), SIDE // 2)
+
+    return level(high) >= level(low)
+
+
 def kernel(
     n_row, n_col, wrapped, col_steps, row_steps, pre, offset,
-    x, m, acc, mcol, tri, own_col, bottom, edge_x, edge_y, left, above, corner,
+    x, sides, m, acc, mcol, tri, own_col, bottom, edge_x, edge_y, left, above, corner,
     jump_x, jump_y, seen_x, seen_y, first_x, first_y,
     in_sem, edge_sem, halo_send, halo_recv, ready_x, ready_y, x_send, x_recv, y_send, y_recv, first_recv,
 ):
@@ -94,7 +102,11 @@
         )
         for k, part in enumerate(PARTS)
     ]
-    for copy in get_parts[:1] + [get_bottom, get_corner] + get_parts[1:]:
+    get_sides = [
+        pltpu.make_async_copy(src.at[:, pl.ds(at, LANES)], sides.at[k], edge_sem.at[2 + k])
+        for k, at in enumerate((0, cols - LANES))
+    ]
+    for copy in [get_sides[0]] + get_parts[:MEET] + [get_bottom, get_corner] + get_parts[MEET:] + [get_sides[1]]:
         copy.start()
 
     barrier = pltpu.get_barrier_semaphore()
@@ -106,52 +118,87 @@
     def _():
         greet({"col": c - 1})
 
-    @pl.when(r > 0)
-    def _():
-        greet({"row": r - 1})
-
     @pl.when((r > 0) & (c > 0))
     def _():
         greet({"row": r - 1, "col": c - 1})
+
+    @pl.loop(0, r)
+    def _(k):
+        at = r - 1 - k
+
+        @pl.when((k == 0) | jnp.logical_not(far_side(at, r)))
+        def _():
+            greet({"row": at})
 
     @pl.loop(r + 1, n_row)
     def _(t):
-        greet({"row": t})
+        @pl.when(far_side(r, t))
+        def _():
+            greet({"row": t})
 
     @pl.loop(c + 1, n_col)
     def _(t):
         greet({"col": t})
 
     has_right, has_below = c < n_col - 1, r < n_row - 1
-    touching = has_right.astype(jnp.int32) + has_below.astype(jnp.int32)
-    touching = touching + (has_right & has_below).astype(jnp.int32)
+    expected = c + has_right.astype(jnp.int32) + (has_right & has_below).astype(jnp.int32)
+    for k in range(n_row):
+        from_low = (k < r) & far_side(k, r)
+        from_high = (k == r + 1) | ((k > r) & jnp.logical_not(far_side(r, k)))
+        expected = expected + (from_low | from_high).astype(jnp.int32)
 
     def meet():
-        pl.semaphore_wait(barrier, r + c + touching)
-
-        @pl.loop(0, r)
+        get_bottom.wait()
+        get_corner.wait()
+        down_total = down[7:8, LANES - 1 : LANES] - row_steps[0, 0, 0].astype(jnp.float32)
+        for s in range(8):
+            edge_y[5:6, LANES * s : LANES * (s + 1)] = jnp.broadcast_to(down_total, (1, LANES))
+        pl.semaphore_wait(barrier, expected)
+
+        @pl.when(has_below)
+        def _():
+            to_below.start()
+
+        @pl.when(has_right & has_below)
+        def _():
+            to_both.start()
+
+        @pl.loop(1, r)
         def _(k):
-            pl.semaphore_signal(
-                ready_y.at[r], inc=1, device_id={"row": r - 1 - k}, device_id_type=MESH
-            )
-
-        @pl.loop(0, c)
+            at = r - 1 - k
+
+            @pl.when(far_side(at, r))
+            def _():
+                pl.semaphore_signal(ready_y.at[r], inc=1, device_id={"row": at}, device_id_type=MESH)
+
+        @pl.loop(1, c)
         def _(k):
             pl.semaphore_signal(
                 ready_x.at[c], inc=1, device_id={"col": c - 1 - k}, device_id_type=MESH
             )
+
+    get_sides[0].wait()
+    for s in range(8):
+        own_col[pl.ds(s, 1), :] = sides[0, pl.ds(LANES * s, LANES), :].T[0:1, :]
+    (down,) = running_turns([own_col[...]])
+    def halo(src_ref, dst_ref, k, device):
+        return pltpu.make_async_remote_copy(
+            src_ref=src_ref, dst_ref=dst_ref, send_sem=halo_send.at[k], recv_sem=halo_recv.at[k],
+            device_id=device, device_id_type=MESH,
+        )
+
+    next_row, next_col = lax.rem(r + 1, n_row), lax.rem(c + 1, n_col)
+    to_right = halo(edge_x, left, 0, {"col": next_col})
+    to_below = halo(edge_y.at[pl.ds(5, 3), :], above.at[pl.ds(5, 3), :], 1, {"row": next_row})
+    to_both = halo(bottom, corner, 2, {"row": next_row, "col": next_col})
+    sends = ((has_below, to_below), (has_right, to_right), (has_right & has_below, to_both))
+    arrivals = ((r > 0, to_below), (c > 0, to_right), ((r > 0) & (c > 0), to_both))
 
     first = 0
     for k, part in enumerate(PARTS):
         if k == MEET:
             meet()
         get_parts[k].wait()
-        for s in range(first // LANES, (first + part) // LANES):
-            at = pl.ds(LANES * s, LANES)
-            own_col[pl.ds(s, 1), :] = x[at, pl.ds(0, LANES)].T[0:1, :]
-            turned = x[at, pl.ds(cols - LANES, LANES)].T
-            edge_x[pl.ds(s, 1), :] = turned[LANES - 2 : LANES - 1, :]
-            edge_x[pl.ds(8 + s, 1), :] = turned[LANES - 1 : LANES, :]
         for q in range(first // STRIP, (first + part) // STRIP):
             at = pl.ds(STRIP * q, STRIP)
             lane = lax.broadcasted_iota(jnp.int32, (STRIP, LANES), 1)
@@ -169,6 +216,12 @@
             acc[at, :] = counts[0].astype(jnp.bfloat16)
         first += part
 
+    get_sides[1].wait()
+    for s in range(8):
+        turned = sides[1, pl.ds(LANES * s, LANES), :].T
+        edge_x[pl.ds(s, 1), :] = turned[LANES - 2 : LANES - 1, :]
+        edge_x[pl.ds(8 + s, 1), :] = turned[LANES - 1 : LANES, :]
+
     sub, lane = positions((8, LANES))
     flat_totals = lax.dot_general(
         jnp.ones((8, LANES), jnp.bfloat16), acc[...], (((1,), (1,)), ((), ())),
@@ -177,31 +230,102 @@
     row_totals = jnp.zeros((8, LANES), jnp.float32)
     for s in range(8):
         row_totals = jnp.where(sub == s, flat_totals[:, LANES * s : LANES * (s + 1)], row_totals)
-    (down,) = running_turns([own_col[...]])
     edge_x[16:24, :] = down + row_totals - col_steps[0, 0, 0].astype(jnp.float32)
-    get_bottom.wait()
-    get_corner.wait()
-    down_total = down[7:8, LANES - 1 : LANES] - row_steps[0, 0, 0].astype(jnp.float32)
-    for s in range(8):
-        edge_y[5:6, LANES * s : LANES * (s + 1)] = jnp.broadcast_to(down_total, (1, LANES))
-
-    def halo(src_ref, dst_ref, k, device):
-        return pltpu.make_async_remote_copy(
-            src_ref=src_ref, dst_ref=dst_ref, send_sem=halo_send.at[k], recv_sem=halo_recv.at[k],
-            device_id=device, device_id_type=MESH,
-        )
-
-    next_row, next_col = lax.rem(r + 1, n_row), lax.rem(c + 1, n_col)
-    to_right = halo(edge_x, left, 0, {"col": next_col})
-    to_below = halo(edge_y.at[pl.ds(5, 3), :], above.at[pl.ds(5, 3), :], 1, {"row": next_row})
-    to_both = halo(bottom, corner, 2, {"row": next_row, "col": next_col})
-    sends = ((has_below, to_below), (has_right, to_right), (has_right & has_below, to_both))
-    arrivals = ((r > 0, to_below), (c > 0, to_right), ((r > 0) & (c > 0), to_both))
-
-    for holds, copy in sends:
+    @pl.when(has_right)
+    def _():
+        to_right.start()
+
+    for holds, copy in arrivals:
         @pl.when(holds)
         def _(copy=copy):
-            copy.start()
+            copy.wait_recv()
+
+    col0, row0 = own_col[...], row_line(x, 0)
+    col_in, col_out = left[0:8, :], left[8:16, :]
+    row_in, row_out = row_line(above, 6), row_line(above, 7)
+    weight_x = edge_weight(
+        col_in, col_out, corner[7:8, LANES - 2 : LANES - 1], corner[7:8, LANES - 1 : LANES], r == 0
+    )
+    weight_y = edge_weight(
+        row_in, row_out, corner[6:7, LANES - 1 : LANES], corner[7:8, LANES - 1 : LANES], c == 0
+    )
+    along, along_above = running_turns([row0, row_out])
+    miss_x = down - left[16:24, :] - turns(col0 - col_out)
+    miss_y = along - along_above - above[5:6, 0:LANES] - turns(row0 - row_out)
+    mean_x = total(weight_x * miss_x) / total(weight_x)
+    mean_y = total(weight_y * miss_y) / total(weight_y)
+    jump_x[...] = jnp.broadcast_to(jnp.where(c == 0, 0.0, mean_x), (8, LANES))
+    jump_y[...] = jnp.broadcast_to(jnp.where(r == 0, 0.0, mean_y), (8, LANES))
+
+    def to_row(t):
+        return pltpu.make_async_remote_copy(
+            src_ref=jump_y.at[pl.ds(0, 1), :], dst_ref=seen_y.at[pl.ds(r, 1), :],
+            send_sem=y_send.at[t], recv_sem=y_recv.at[r],
+            device_id={"row": t}, device_id_type=MESH,
+        )
+
+    def to_col(t):
+        return pltpu.make_async_remote_copy(
+            src_ref=jump_x.at[pl.ds(0, 1), :], dst_ref=seen_x.at[pl.ds(c, 1), :],
+            send_sem=x_send.at[t], recv_sem=x_recv.at[c],
+            device_id={"col": t}, device_id_type=MESH,
+        )
+
+    def from_row(k):
+        return pltpu.make_async_remote_copy(
+            src_ref=jump_y.at[pl.ds(0, 1), :], dst_ref=seen_y.at[pl.ds(k, 1), :],
+            send_sem=y_send.at[k], recv_sem=y_recv.at[k],
+            device_id={"row": k}, device_id_type=MESH,
+        )
+
+    def from_col(k):
+        return pltpu.make_async_remote_copy(
+            src_ref=jump_x.at[pl.ds(0, 1), :], dst_ref=seen_x.at[pl.ds(k, 1), :],
+            send_sem=x_send.at[k], recv_sem=x_recv.at[k],
+            device_id={"col": k}, device_id_type=MESH,
+        )
+
+    def first_row(t):
+        return pltpu.make_async_remote_copy(
+            src_ref=jump_y.at[pl.ds(0, 1), :], dst_ref=first_y.at[pl.ds(0, 1), :],
+            send_sem=y_send.at[t], recv_sem=first_recv.at[0],
+            device_id={"row": t}, device_id_type=MESH,
+        )
+
+    def first_col(t):
+        return pltpu.make_async_remote_copy(
+            src_ref=jump_x.at[pl.ds(0, 1), :], dst_ref=first_x.at[pl.ds(0, 1), :],
+            send_sem=x_send.at[t], recv_sem=first_recv.at[1],
+            device_id={"col": t}, device_id_type=MESH,
+        )
+
+    def await_y(t):
+        @pl.when((t > r + 1) & far_side(r, t))
+        def _():
+            pl.semaphore_wait(ready_y.at[t], 1)
+
+    def await_x(t):
+        @pl.when(t > c + 1)
+        def _():
+            pl.semaphore_wait(ready_x.at[t], 1)
+
+    def send_y(t):
+        await_y(t)
+        to_row(t).start()
+
+    def send_x(t):
+        await_x(t)
+        to_col(t).start()
+
+    stop_x = jnp.where(c < n_col // 4, n_col // 2, n_col)
+    start_y, start_x = jnp.where(r == 0, n_row, r + 1), jnp.where(c == 0, stop_x, c + 1)
+    near_y, near_x = jnp.minimum(start_y + NEAR, n_row), jnp.minimum(start_x + NEAR, stop_x)
+    pl.loop(start_y, near_y)(send_y)
+    pl.loop(start_x, near_x)(send_x)
+    late_x = jnp.where(c < n_col // 2, near_x, stop_x)
+    pl.loop(near_x, late_x)(send_x)
+    pl.loop(near_y, n_row)(send_y)
+    pl.loop(late_x, stop_x)(send_x)
 
     for s in range(8):
         mcol[pl.ds(LANES * s, LANES), :] = jnp.broadcast_to(down[s : s + 1, :], (LANES, LANES)).T
@@ -222,86 +346,6 @@
                 pre[at, here] = x[at, here] * PER_CYCLE - counted[:, LANES * h : LANES * (h + 1)] - base
             base = base + counted[:, 2 * LANES :]
 
-    for holds, copy in arrivals:
-        @pl.when(holds)
-        def _(copy=copy):
-            copy.wait_recv()
-
-    col0, row0 = own_col[...], row_line(x, 0)
-    col_in, col_out = left[0:8, :], left[8:16, :]
-    row_in, row_out = row_line(above, 6), row_line(above, 7)
-    weight_x = edge_weight(
-        col_in, col_out, corner[7:8, LANES - 2 : LANES - 1], corner[7:8, LANES - 1 : LANES], r == 0
-    )
-    weight_y = edge_weight(
-        row_in, row_out, corner[6:7, LANES - 1 : LANES], corner[7:8, LANES - 1 : LANES], c == 0
-    )
-    along, along_above = running_turns([row0, row_out])
-    miss_x = down - left[16:24, :] - turns(col0 - col_out)
-    miss_y = along - along_above - above[5:6, 0:LANES] - turns(row0 - row_out)
-    mean_x = total(weight_x * miss_x) / total(weight_x)
-    mean_y = total(weight_y * miss_y) / total(weight_y)
-    jump_x[...] = jnp.broadcast_to(jnp.where(c == 0, 0.0, mean_x), (8, LANES))
-    jump_y[...] = jnp.broadcast_to(jnp.where(r == 0, 0.0, mean_y), (8, LANES))
-
-    def to_row(t):
-        return pltpu.make_async_remote_copy(
-            src_ref=jump_y.at[pl.ds(0, 1), :], dst_ref=seen_y.at[pl.ds(r, 1), :],
-            send_sem=y_send.at[t], recv_sem=y_recv.at[r],
-            device_id={"row": t}, device_id_type=MESH,
-        )
-
-    def to_col(t):
-        return pltpu.make_async_remote_copy(
-            src_ref=jump_x.at[pl.ds(0, 1), :], dst_ref=seen_x.at[pl.ds(c, 1), :],
-            send_sem=x_send.at[t], recv_sem=x_recv.at[c],
-            device_id={"col": t}, device_id_type=MESH,
-        )
-
-    def from_row(k):
-        return pltpu.make_async_remote_copy(
-            src_ref=jump_y.at[pl.ds(0, 1), :], dst_ref=seen_y.at[pl.ds(k, 1), :],
-            send_sem=y_send.at[k], recv_sem=y_recv.at[k],
-            device_id={"row": k}, device_id_type=MESH,
-        )
-
-    def from_col(k):
-        return pltpu.make_async_remote_copy(
-            src_ref=jump_x.at[pl.ds(0, 1), :], dst_ref=seen_x.at[pl.ds(k, 1), :],
-            send_sem=x_send.at[k], recv_sem=x_recv.at[k],
-            device_id={"col": k}, device_id_type=MESH,
-        )
-
-    def first_row(t):
-        return pltpu.make_async_remote_copy(
-            src_ref=jump_y.at[pl.ds(0, 1), :], dst_ref=first_y.at[pl.ds(0, 1), :],
-            send_sem=y_send.at[t], recv_sem=first_recv.at[0],
-            device_id={"row": t}, device_id_type=MESH,
-        )
-
-    def first_col(t):
-        return pltpu.make_async_remote_copy(
-            src_ref=jump_x.at[pl.ds(0, 1), :], dst_ref=first_x.at[pl.ds(0, 1), :],
-            send_sem=x_send.at[t], recv_sem=first_recv.at[1],
-            device_id={"col": t}, device_id_type=MESH,
-        )
-
-    def send_y(t):
-        pl.semaphore_wait(ready_y.at[t], 1)
-        to_row(t).start()
-
-    def send_x(t):
-        pl.semaphore_wait(ready_x.at[t], 1)
-        to_col(t).start()
-
-    stop_x = jnp.where(c < n_col // 4, n_col // 2, n_col)
-    start_y, start_x = jnp.where(r == 0, n_row, r + 1), jnp.where(c == 0, stop_x, c + 1)
-    near_y, near_x = jnp.minimum(start_y + NEAR, n_row), jnp.minimum(start_x + NEAR, stop_x)
-    pl.loop(start_y, near_y)(send_y)
-    pl.loop(start_x, near_x)(send_x)
-    pl.loop(near_y, n_row)(send_y)
-    pl.loop(near_x, stop_x)(send_x)
-
     @pl.loop(1, r)
     def _(k):
         from_row(k).wait_recv()
@@ -321,7 +365,7 @@
 
         @pl.loop(1, n_row)
         def _(t):
-            pl.semaphore_wait(ready_y.at[t], 1)
+            await_y(t)
             first_row(t).start()
 
     @pl.when(c == 0)
@@ -330,7 +374,7 @@
 
         @pl.loop(1, n_col)
         def _(t):
-            pl.semaphore_wait(ready_x.at[t], 1)
+            await_x(t)
             first_col(t).start()
 
     @pl.when(c > 0)
@@ -401,6 +445,7 @@
         out_specs=(in_vmem, in_vmem),
         scratch_shapes=[
             pltpu.VMEM((rows, cols), f32),
+            pltpu.VMEM((2, rows, LANES), f32),
             pltpu.VMEM((cols // LANES, rows, LANES), jnp.bfloat16),
             pltpu.VMEM((rows, LANES), jnp.bfloat16),
             pltpu.VMEM((rows, LANES), f32),
@@ -419,7 +464,7 @@
             line,
             line,
             dma((len(PARTS),)),
-            dma((2,)),
+            dma((4,)),
             dma((3,)),
             dma((3,)),
             pltpu.SemaphoreType.REGULAR((n_col,)),

time: 18.1 us -> 17.6 us (0.972); the launches traced: 18 us -> 17.3 us
  Pallas kernels: 16.7 us -> 16 us
    pallas_call x1, Pallas kernels: 14.6 us -> 13.8 us  [on_device(): pl.pallas_call(functools.partial(kernel, n_row, n_col), out_shape=(jax.Sh...]
where the time goes in v4:
time: 17.6 us; the launch traced here: 17.3 us
  Pallas kernels  16 us (91%)
  between operations  1.3 us (7%)
    pallas_call x1, Pallas kernels, on_device(): pl.pallas_call(functools.partial(kernel, n_row, n_col), out_shape=(jax.Sh...  13.8 us
    pallas_call x1, Pallas kernels, on_device(): pl.pallas_call(add_offset, out_shape=jax.ShapeDtypeStruct((1, rows, cols)...  2.14 us

profile of v4, /device:TPU:38, one launch (start us, length us, event | category | flops | bytes accessed | tf_op | source)
XLA Modules:
  0.0 17.3 jit_solution(7421850708823039985)
XLA Ops:
  1.3 13.8 %shard_map.37 = (f32[1024,1024]{1,0:T(8,128)S(1)}, f32[8,128]{1,0:T(8,128)S(1)}) custom-call(f32[1,1024,1024]{2,1,0:T(8,128)} %wrapped.1, s32[1,1,1]{2,1,0:T(1,128)S(6)} %copy.4.col_steps, s32[1,1,1]{2,1,0:T(1,128)S(6)} %copy.5.row_steps), custom_call_target="tpu_custom_call" | custom-call | tf_op jit(solution)/shard_map/pallas_call | solution.py:441
  15.1 2.1 %shard_map.38 = f32[1,1024,1024]{2,1,0:T(8,128)} custom-call(f32[1024,1024]{1,0:T(8,128)S(1)} %get-tuple-element.7.pre, f32[8,128]{1,0:T(8,128)S(1)} %get-tuple-element.8.offset), custom_call_target="tpu_custom_call" | custom-call | tf_op jit(solution)/shard_map/pallas_call | solution.py:482

commit v5 on v4

--- a/solution.py
+++ b/solution.py
@@ -74,11 +74,8 @@
     return jnp.concatenate([ref[i : i + 1, LANES * s : LANES * (s + 1)] for s in range(8)], axis=0)
 
 
-def far_side(low, high):
-    def level(t):
-        return jnp.minimum(lax.div(t, SIDE), SIDE // 2) + jnp.minimum(lax.rem(t, SIDE), SIDE // 2)
-
-    return level(high) >= level(low)
+def distance(t):
+    return jnp.minimum(lax.div(t, SIDE), SIDE // 2) + jnp.minimum(lax.rem(t, SIDE), SIDE // 2)
 
 
 def kernel(
@@ -114,6 +111,10 @@
     def greet(device):
         pl.semaphore_signal(barrier, inc=1, device_id=device, device_id_type=MESH)
 
+    away = distance(r)
+    row_distance = [min(t // SIDE, SIDE // 2) + min(t % SIDE, SIDE // 2) for t in range(n_row)]
+    from_low = [(t < r) & (row_distance[t] <= away) for t in range(n_row)]
+
     @pl.when(c > 0)
     def _():
         greet({"col": c - 1})
@@ -122,18 +123,11 @@
     def _():
         greet({"row": r - 1, "col": c - 1})
 
-    @pl.loop(0, r)
-    def _(k):
-        at = r - 1 - k
-
-        @pl.when((k == 0) | jnp.logical_not(far_side(at, r)))
-        def _():
-            greet({"row": at})
-
-    @pl.loop(r + 1, n_row)
-    def _(t):
-        @pl.when(far_side(r, t))
-        def _():
+    for t in range(n_row):
+        greets_low = (t < r) & ((t == r - 1) | (row_distance[t] > away))
+
+        @pl.when(greets_low | ((t > r) & (row_distance[t] >= away)))
+        def _(t=t):
             greet({"row": t})
 
     @pl.loop(c + 1, n_col)
@@ -142,10 +136,9 @@
 
     has_right, has_below = c < n_col - 1, r < n_row - 1
     expected = c + has_right.astype(jnp.int32) + (has_right & has_below).astype(jnp.int32)
-    for k in range(n_row):
-        from_low = (k < r) & far_side(k, r)
-        from_high = (k == r + 1) | ((k > r) & jnp.logical_not(far_side(r, k)))
-        expected = expected + (from_low | from_high).astype(jnp.int32)
+    for t in range(n_row):
+        from_high = (t == r + 1) | ((t > r) & (row_distance[t] < away))
+        expected = expected + (from_low[t] | from_high).astype(jnp.int32)
 
     def meet():
         get_bottom.wait()
@@ -163,13 +156,10 @@
         def _():
             to_both.start()
 
-        @pl.loop(1, r)
-        def _(k):
-            at = r - 1 - k
-
-            @pl.when(far_side(at, r))
-            def _():
-                pl.semaphore_signal(ready_y.at[r], inc=1, device_id={"row": at}, device_id_type=MESH)
+        for t in reversed(range(n_row)):
+            @pl.when(from_low[t] & (t != r - 1))
+            def _(t=t):
+                pl.semaphore_signal(ready_y.at[r], inc=1, device_id={"row": t}, device_id_type=MESH)
 
         @pl.loop(1, c)
         def _(k):
@@ -300,7 +290,7 @@
         )
 
     def await_y(t):
-        @pl.when((t > r + 1) & far_side(r, t))
+        @pl.when((t > r + 1) & (away <= distance(t)))
         def _():
             pl.semaphore_wait(ready_y.at[t], 1)
 

time: 17.6 us -> 17.6 us (level)
  the two profiles are of different devices: /device:TPU:38 before, /device:TPU:166 now
where the time goes in v5:
time: 17.6 us; the launch traced here: 17.5 us
  Pallas kernels  16.2 us (92%)
  between operations  1.3 us (7%)
    pallas_call x1, Pallas kernels, on_device(): pl.pallas_call(functools.partial(kernel, n_row, n_col), out_shape=(jax.Sh...  14.1 us
    pallas_call x1, Pallas kernels, on_device(): pl.pallas_call(add_offset, out_shape=jax.ShapeDtypeStruct((1, rows, cols)...  2.14 us

profile of v5, /device:TPU:166, one launch (start us, length us, event | category | flops | bytes accessed | tf_op | source)
XLA Modules:
  0.0 17.5 jit_solution(12252361400785842516)
XLA Ops:
  1.3 14.1 %shard_map.37 = (f32[1024,1024]{1,0:T(8,128)S(1)}, f32[8,128]{1,0:T(8,128)S(1)}) custom-call(f32[1,1024,1024]{2,1,0:T(8,128)} %wrapped.1, s32[1,1,1]{2,1,0:T(1,128)S(6)} %copy.4.col_steps, s32[1,1,1]{2,1,0:T(1,128)S(6)} %copy.5.row_steps), custom_call_target="tpu_custom_call" | custom-call | tf_op jit(solution)/shard_map/pallas_call | solution.py:431
  15.4 2.1 %shard_map.38 = f32[1,1024,1024]{2,1,0:T(8,128)} custom-call(f32[1024,1024]{1,0:T(8,128)S(1)} %get-tuple-element.7.pre, f32[8,128]{1,0:T(8,128)S(1)} %get-tuple-element.8.offset), custom_call_target="tpu_custom_call" | custom-call | tf_op jit(solution)/shard_map/pallas_call | solution.py:472

commit v6 on v5

--- a/solution.py
+++ b/solution.py
@@ -315,7 +315,6 @@
     late_x = jnp.where(c < n_col // 2, near_x, stop_x)
     pl.loop(near_x, late_x)(send_x)
     pl.loop(near_y, n_row)(send_y)
-    pl.loop(late_x, stop_x)(send_x)
 
     for s in range(8):
         mcol[pl.ds(LANES * s, LANES), :] = jnp.broadcast_to(down[s : s + 1, :], (LANES, LANES)).T
@@ -335,6 +334,8 @@
                 here = pl.ds(LANES * (2 * j + h), LANES)
                 pre[at, here] = x[at, here] * PER_CYCLE - counted[:, LANES * h : LANES * (h + 1)] - base
             base = base + counted[:, 2 * LANES :]
+
+    pl.loop(late_x, stop_x)(send_x)
 
     @pl.loop(1, r)
     def _(k):

time: 17.6 us -> 17.5 us (level)
  the two profiles are of different devices: /device:TPU:166 before, /device:TPU:38 now
where the time goes in v6:
time: 17.5 us; the launch traced here: 17.2 us
  Pallas kernels  15.9 us (91%)
  between operations  1.3 us (7%)
    pallas_call x1, Pallas kernels, on_device(): pl.pallas_call(functools.partial(kernel, n_row, n_col), out_shape=(jax.Sh...  13.8 us
    pallas_call x1, Pallas kernels, on_device(): pl.pallas_call(add_offset, out_shape=jax.ShapeDtypeStruct((1, rows, cols)...  2.14 us

profile of v6, /device:TPU:38, one launch (start us, length us, event | category | flops | bytes accessed | tf_op | source)
XLA Modules:
  0.0 17.2 jit_solution(13813290258241943114)
XLA Ops:
  1.3 13.8 %shard_map.37 = (f32[1024,1024]{1,0:T(8,128)S(1)}, f32[8,128]{1,0:T(8,128)S(1)}) custom-call(f32[1,1024,1024]{2,1,0:T(8,128)} %wrapped.1, s32[1,1,1]{2,1,0:T(1,128)S(6)} %copy.4.col_steps, s32[1,1,1]{2,1,0:T(1,128)S(6)} %copy.5.row_steps), custom_call_target="tpu_custom_call" | custom-call | tf_op jit(solution)/shard_map/pallas_call | solution.py:432
  15.1 2.1 %shard_map.38 = f32[1,1024,1024]{2,1,0:T(8,128)} custom-call(f32[1024,1024]{1,0:T(8,128)S(1)} %get-tuple-element.7.pre, f32[8,128]{1,0:T(8,128)S(1)} %get-tuple-element.8.offset), custom_call_target="tpu_custom_call" | custom-call | tf_op jit(solution)/shard_map/pallas_call | solution.py:473
